TPU v7x, 128 devices: a whole 4x4x4 slice. The times are simulated.
128 devices in a mesh: rows: 8 (over x, core), cols: 16 (over z, y).
Axes of the slice: x: 4, y: 4, z: 4, core: 2. Of those that a mesh axis runs over, the one named last changes fastest.
Arguments:
- samples: bfloat16 [4096, 65536], P('rows', 'cols'), may hold values from -0.0234375 to 0.0234375
- labels: int32 [4096], P('rows'), may hold values 0 or 1
- weights: float32 [65536], P('cols'), may hold values from -7 to 7, as said below
- hist_s: float32 [16, 65536], P(None, 'cols'), may hold values from -60 to 60
- hist_y: float32 [16, 65536], P(None, 'cols'), may hold values from -480 to 480, as said below
- counter: int32 [1], replicated, may hold values from 0 to 4095
Outputs:
- new_weights: float32 [65536], P('cols')
- gradient: float32 [65536], P('cols')
Inputs may be any that keep to these rules, and one draw needn't show every extreme that they name: weights share a common direction with the rows of hist_s. Each entry of hist_y[j] is a positive multiple of the same entry of hist_s[j], so s_j . y_j > 0.
All inputs are finite; a program needn't handle non-finite values. No bound on the sum of `labels` on one device may be relied on, other than what follows from the above.
Results may differ from a plain program's by a relative error of at most 0.0013.
Values sent between devices are 32-bit elements; how exact they have to be, the bound alone decides.
No kernel may reach another device: no remote copies, remote signals or barrier semaphores. Data moves between devices by JAX's collectives and lax.ppermute only.
A program may use at most 64 MiB of HBM per device.

v0:
```python
import jax
import jax.numpy as jnp
from jax import lax
from jax.sharding import Mesh
from jax.sharding import PartitionSpec as P

HIST = 16
ROWS = ("rows_0", "rows_1")
COLS = ("cols_0", "cols_1")


penalty = 4.0
step_length = 0.5
highest = lax.Precision.HIGHEST


def from_everyone(array, axis):
    copies = jnp.broadcast_to(array, (lax.axis_size(axis), *array.shape))
    return lax.all_to_all(copies, axis, split_axis=0, concat_axis=0, tiled=True)


def taken_together(array, axis):
    everything = from_everyone(array, axis)
    return jnp.sum(everything, axis=0)


def one_axis_at_a_time(array, axes):
    far, near = axes
    return taken_together(taken_together(array, near), far)


def in_one(arrays, axis):
    line, at, done = (jnp.concatenate([a.reshape(-1) for a in arrays]), 0, [])
    running = one_axis_at_a_time(line, axis)
    for a in arrays:
        done.append(running[at : at + a.size].reshape(a.shape))
        at += a.size
    return tuple(done)


def row_share(values):
    width = values.shape[-1] // lax.axis_size(ROWS)
    return lax.dynamic_slice_in_dim(values, lax.axis_index(ROWS) * width, width, values.ndim - 1)


def quad_form(left, matrix, right):
    return jnp.dot(left, jnp.dot(matrix, right, precision=highest), precision=highest)


def gram_recursion(gram, basis, newest):
    count = 2 * HIST + 1
    places = jnp.arange(count, dtype=jnp.int32)
    select_s = (places == newest).astype(jnp.float32)
    select_y = (places == newest + HIST).astype(jnp.float32)
    gamma = quad_form(select_s, gram, select_y) / quad_form(select_y, gram, select_y)
    weights_of = (places == 2 * HIST).astype(jnp.float32)
    coefs = []
    pairs = []
    for step in range(HIST):
        slot = (newest - step) % HIST
        pick_s = (places == slot).astype(jnp.float32)
        pick_y = (places == slot + HIST).astype(jnp.float32)
        rho = 1.0 / quad_form(pick_s, gram, pick_y)
        coef = rho * quad_form(pick_s, gram, weights_of)
        coefs.append(coef)
        pairs.append((pick_s, pick_y, rho))
        weights_of = weights_of - coef * pick_y
    result_of = gamma * weights_of
    for step in reversed(range(HIST)):
        pick_s, pick_y, rho = pairs[step]
        beta = rho * quad_form(pick_y, gram, result_of)
        result_of = result_of + (coefs[step] - beta) * pick_s
    return jnp.dot(result_of, basis, precision=highest)


def body(samples, labels, weights, hist_s, hist_y, counter):
    margin_part = jnp.dot(samples, weights.astype(jnp.bfloat16), preferred_element_type=jnp.float32)
    margin = taken_together(margin_part, COLS)
    resid = (jax.nn.sigmoid(margin) - labels.astype(jnp.float32)).astype(jnp.bfloat16)
    total_part = jnp.dot(resid, samples, preferred_element_type=jnp.float32)
    newest = counter[0] % HIST
    history = jnp.concatenate([hist_s, hist_y], axis=0)
    narrow_hist = row_share(history)
    hist_part = jnp.dot(
        narrow_hist, narrow_hist.T, precision=highest, preferred_element_type=jnp.float32
    )
    lead = weights / lax.axis_size(ROWS) + penalty * total_part
    cross_part = jnp.dot(history, lead, precision=highest, preferred_element_type=jnp.float32)
    hist_gram, cross = in_one((hist_part, cross_part), (("rows_0", "rows_1"), ("cols_0", "cols_1")))
    total = taken_together(total_part, ROWS)
    gradient = weights + penalty * total
    top = jnp.concatenate([hist_gram, cross[:, None]], axis=1)
    corner = jnp.concatenate([cross, jnp.zeros((1,), jnp.float32)], axis=0)
    gram = jnp.concatenate([top, corner[None, :]], axis=0)
    basis = jnp.concatenate([history, gradient[None, :]], axis=0)
    result = gram_recursion(gram, basis, newest)
    return (weights - step_length * result, gradient)


def solution(mesh):
    split = Mesh(mesh.devices.reshape(4, 2, 4, 4), ("rows_0", "rows_1", "cols_0", "cols_1"))
    return jax.shard_map(
        body,
        mesh=split,
        in_specs=(P(ROWS, COLS), P(ROWS), P(COLS), P(None, COLS), P(None, COLS), P()),
        out_specs=(P(COLS), P(COLS)),
        check_vma=False,
    )
```

profile of v0, /device:TPU:1, one launch (start us, length us, event | category | flops | bytes accessed | tf_op | source)
XLA Modules:
  0.0 129.1 jit_solution(1960840014889588994)
XLA Ops:
  1.5 3.4 %fusion.192 = f32[1,512]{1,0:T(1,128)S(1)} fusion(bf16[512,4096]{1,0:T(8,128)(2,1)} %param.6, bf16[4096,1]{0,1:T(2,128)(2,1)S(1)} %reshape.36), kind=kOutput, calls=%fused_computation.316 | convolution fusion | flops 4194304 | bytes 4204544 | tf_op jit(solution)/shard_map/dot_general | solution.py:77
  5.5 8.6 %all-to-all-start = ((f32[16,1,512]{2,1,0:T(1,128)}), f32[16,1,512]{2,1,0:T(1,128)S(1)}, u32[]{:S(2)}, u32[]{:S(2)}) async-start(f32[16,1,512]{2,1,0:T(1,128)} %broadcast_in_dim.21), calls=%async_computation | async-start | bytes 65536 | tf_op jit(solution)/shard_map/all_to_all | solution.py:19
  14.1 6.4 %all-to-all-done = f32[16,1,512]{2,1,0:T(1,128)S(1)} async-done(((f32[16,1,512]{2,1,0:T(1,128)}), f32[16,1,512]{2,1,0:T(1,128)S(1)}, u32[]{:S(2)}, u32[]{:S(2)}) %all-to-all-start) | async-done | bytes 32800 | tf_op jit(solution)/shard_map/all_to_all | solution.py:19
  20.6 2.8 %fusion.193 = f32[1,4096]{1,0:T(1,128)S(1)} fusion(bf16[512,1]{0,1:T(2,128)(2,1)S(1)} %reshape.38, bf16[512,4096]{1,0:T(8,128)(2,1)} %param.6), kind=kOutput, calls=%fused_computation.317 | convolution fusion | flops 4194304 | bytes 4211712 | tf_op jit(solution)/shard_map/dot_general | solution.py:80
  24.2 6.4 %all-to-all-start.3 = ((f32[8,1,4096]{2,1,0:T(1,128)}), f32[8,1,4096]{2,1,0:T(1,128)S(1)}, u32[]{:S(2)}, u32[]{:S(2)}) async-start(f32[8,1,4096]{2,1,0:T(1,128)} %broadcast_in_dim.26), calls=%async_computation.3 | async-start | bytes 262144 | tf_op jit(solution)/shard_map/all_to_all | solution.py:19
  30.9 4.9 %all-to-all-done.3 = f32[8,1,4096]{2,1,0:T(1,128)S(1)} async-done(((f32[8,1,4096]{2,1,0:T(1,128)}), f32[8,1,4096]{2,1,0:T(1,128)S(1)}, u32[]{:S(2)}, u32[]{:S(2)}) %all-to-all-start.3) | async-done | bytes 131104 | tf_op jit(solution)/shard_map/all_to_all | solution.py:19
  36.5 9.3 %all_to_all.24 = f32[16,1,1056]{2,1,0:T(1,128)S(1)} all-to-all(f32[16,1,1056]{2,1,0:T(1,128)S(1)} %broadcast_in_dim.22), channel_id=1, replica_groups=mesh['rows_0'=4,'rows_1'=2,'cols_0'=4,'cols_1'=4] {'cols_0','cols_1'}, dimensions={0} | all-to-all | bytes 135168 | tf_op jit(solution)/shard_map/all_to_all | solution.py:19
  46.5 5.5 %all-to-all-start.2 = ((f32[8,1,1056]{2,1,0:T(1,128)}), f32[8,1,1056]{2,1,0:T(1,128)S(1)}, u32[]{:S(2)}, u32[]{:S(2)}) async-start(f32[8,1,1056]{2,1,0:T(1,128)} %broadcast_in_dim.23), calls=%async_computation.2 | async-start | bytes 73728 | tf_op jit(solution)/shard_map/all_to_all | solution.py:19
  53.1 3.7 %all-to-all-done.2 = f32[8,1,1056]{2,1,0:T(1,128)S(1)} async-done(((f32[8,1,1056]{2,1,0:T(1,128)}), f32[8,1,1056]{2,1,0:T(1,128)S(1)}, u32[]{:S(2)}, u32[]{:S(2)}) %all-to-all-start.2) | async-done | bytes 33824 | tf_op jit(solution)/shard_map/all_to_all | solution.py:19
  58.0 0.8 fusion.127
  63.7 0.8 fusion.59
  66.6 0.8 fusion.61
  69.4 0.8 fusion.63
  72.3 0.8 fusion.65
  75.2 0.8 fusion.67
  78.0 0.8 fusion.69
  80.9 0.8 fusion.71
  83.7 0.8 fusion.73
  86.6 0.8 fusion.75
  89.5 0.8 fusion.77
  92.3 0.8 fusion.79
  95.2 0.8 fusion.81
  98.1 0.8 fusion.83
  100.9 0.8 fusion.85
  (85 shorter events, 31.3 us)
Async XLA Ops:
  0.6 13.5 %copy-start.1 = (f32[16,4096]{1,0:T(8,128)S(1)}, f32[16,4096]{1,0:T(8,128)}, u32[]{:S(2)}) copy-start(f32[16,4096]{1,0:T(8,128)} %param.9) | copy-start | bytes 786436
  0.6 20.0 %copy-start.4 = (s32[512]{0:T(512)S(1)}, s32[512]{0:T(512)}, u32[]{:S(2)}) copy-start(s32[512]{0:T(512)} %param.7) | copy-start | bytes 6148
  1.4 29.1 %copy-start = (f32[16,4096]{1,0:T(8,128)S(1)}, f32[16,4096]{1,0:T(8,128)}, u32[]{:S(2)}) copy-start(f32[16,4096]{1,0:T(8,128)} %param.10) | copy-start | bytes 786436
  1.4 34.5 %copy-start.2 = (f32[4096]{0:T(1024)S(1)}, f32[4096]{0:T(1024)}, u32[]{:S(2)}) copy-start(f32[4096]{0:T(1024)} %param.8) | copy-start | bytes 49156
  5.5 15.1 %all-to-all-start = ((f32[16,1,512]{2,1,0:T(1,128)}), f32[16,1,512]{2,1,0:T(1,128)S(1)}, u32[]{:S(2)}, u32[]{:S(2)}) async-start(f32[16,1,512]{2,1,0:T(1,128)} %broadcast_in_dim.21), calls=%async_computation | async-start | bytes 65536 | tf_op jit(solution)/shard_map/all_to_all | solution.py:19
  24.2 11.6 %all-to-all-start.3 = ((f32[8,1,4096]{2,1,0:T(1,128)}), f32[8,1,4096]{2,1,0:T(1,128)S(1)}, u32[]{:S(2)}, u32[]{:S(2)}) async-start(f32[8,1,4096]{2,1,0:T(1,128)} %broadcast_in_dim.26), calls=%async_computation.3 | async-start | bytes 262144 | tf_op jit(solution)/shard_map/all_to_all | solution.py:19
  35.9 93.2 %copy-start.3 = (f32[4096]{0:T(1024)}, f32[4096]{0:T(1024)S(1)}, u32[]{:S(2)}) copy-start(f32[4096]{0:T(1024)S(1)} %get-tuple-element.5) | copy-start | bytes 49156
  46.5 10.3 %all-to-all-start.2 = ((f32[8,1,1056]{2,1,0:T(1,128)}), f32[8,1,1056]{2,1,0:T(1,128)S(1)}, u32[]{:S(2)}, u32[]{:S(2)}) async-start(f32[8,1,1056]{2,1,0:T(1,128)} %broadcast_in_dim.23), calls=%async_computation.2 | async-start | bytes 73728 | tf_op jit(solution)/shard_map/all_to_all | solution.py:19
where the time goes:
time: 130 us; the launch traced here: 129 us
  matrix products  44.6 us (34%)
  between operations  34.9 us (27%)
  starting transfers between devices  20.5 us (16%)
  waiting for transfers between devices  15.1 us (12%)
  blocking collectives  9.32 us (7%)
  local copies, waits for them, and re-layouts  2.35 us (2%)
  other arithmetic  2.35 us (2%)
    dot_general x49, matrix products, quad_form(): jnp.dot(matrix, right, precision=highest)  37.2 us
    all_to_all x3, starting transfers between devices, from_everyone(): return lax.all_to_all(copies, axis, split_axis=0, concat_axis=0, tiled=True)  20.5 us
    all_to_all x3, waiting for transfers between devices, from_everyone(): return lax.all_to_all(copies, axis, split_axis=0, concat_axis=0, tiled=True)  15.1 us
    all_to_all x1, blocking collectives, from_everyone(): return lax.all_to_all(copies, axis, split_axis=0, concat_axis=0, tiled=True)  9.32 us
    dot_general x1, matrix products, body(): jnp.dot(samples, weights.astype(jnp.bfloat16), preferred_element_type=jnp...  3.41 us
    dot_general x1, matrix products, body(): total_part = jnp.dot(resid, samples, preferred_element_type=jnp.float32)  2.84 us
  transfers between devices with their start and end apart: 3, of which 3 were waited for; matrix products, arithmetic and copies ran while one was open for 0% of the time, Pallas kernels for 0%

commit v1 on v0

v1 whole, which is shorter than its diff:
```python
import jax
import jax.numpy as jnp
from jax import lax
from jax.experimental import pallas as pl
from jax.experimental.pallas import tpu as pltpu
from jax.sharding import PartitionSpec as P

HIST = 16
ROWS = "rows"
COLS = "cols"
CHUNKS = 8

penalty = 4.0
step_length = 0.5
f32 = jnp.float32
bf16 = jnp.bfloat16
highest = lax.Precision.HIGHEST


def iota(shape, axis):
    return lax.broadcasted_iota(jnp.int32, shape, axis)


def dot_t(left, right):
    return lax.dot_general(left, right, (((1,), (1,)), ((), ())), preferred_element_type=f32)


def first_kernel(s_hbm, w_hbm, hs_hbm, hy_hbm, samp, hist, wrow, part, sems):
    feats = samp.shape[1]
    width = feats // CHUNKS
    copies = [
        pltpu.make_async_copy(hs_hbm, hist.at[pl.ds(0, HIST), :], sems.at[0]),
        pltpu.make_async_copy(hy_hbm, hist.at[pl.ds(HIST, HIST), :], sems.at[1]),
        pltpu.make_async_copy(w_hbm, wrow, sems.at[2]),
    ]
    for c in range(CHUNKS):
        cols = pl.ds(c * width, width)
        copies.append(pltpu.make_async_copy(s_hbm.at[:, cols], samp.at[:, cols], sems.at[3 + c]))
    for copy in copies:
        copy.start()
    for copy in copies[:3]:
        copy.wait()
    h = hist[...]
    high = h.astype(bf16)
    low = (h - high.astype(f32)).astype(bf16)
    y_high = high[HIST:]
    y_low = low[HIST:]
    right = jnp.concatenate([y_high] * 8 + [y_low] * 8, axis=0)
    left = jnp.concatenate([high, low], axis=0)
    both = dot_t(left, right)
    gram = (both[:32, 128:] + both[32:, :128]) + both[:32, :128]
    mask = iota((32, 128), 1) // HIST == iota((32, 128), 0) % 8
    gram = jnp.where(mask, gram, 0.0)
    packed = [jnp.sum(gram[8 * a : 8 * a + 8], axis=0, keepdims=True) for a in range(4)]

    acc = jnp.zeros((16, samp.shape[0]), f32)
    for c in range(CHUNKS):
        copies[3 + c].wait()
        cols = slice(c * width, (c + 1) * width)
        w16 = jnp.broadcast_to(wrow[:, cols].astype(bf16), (16, width))
        acc = acc + dot_t(w16, samp[:, cols])
    rows = [acc[0:1, 128 * i : 128 * i + 128] for i in range(4)]
    mine = jnp.concatenate(rows + packed, axis=0)
    part[...] = jnp.broadcast_to(mine[None], part.shape)


def second_kernel(parts, labels, samp, hist, wrow, total, cross, gram):
    summed = jnp.sum(parts[...], axis=0)
    gram[...] = summed
    margin = jnp.concatenate([summed[i : i + 1] for i in range(4)], axis=1)
    resid = (jax.nn.sigmoid(margin) - labels[...].astype(f32)).astype(bf16)
    resid16 = jnp.broadcast_to(resid, (16, resid.shape[1]))
    feats = samp.shape[1]
    width = 512
    acc = jnp.zeros((2 * HIST, 128), f32)
    for c in range(feats // width):
        cols = slice(c * width, (c + 1) * width)
        t = jnp.dot(resid16, samp[:, cols], preferred_element_type=f32)[0:1]
        total[:, cols] = t
        lead = wrow[:, cols] * 0.125 + penalty * t
        prod = hist[:, cols] * lead
        for k in range(width // 128):
            acc = acc + prod[:, 128 * k : 128 * k + 128]
    square = jnp.concatenate([acc, jnp.zeros((96, 128), f32)], axis=0)
    line = jnp.sum(square.T, axis=0, keepdims=True)
    cross[...] = jnp.broadcast_to(line[None], cross.shape)


def solve_kernel(counter, gram, out):
    newest = lax.rem(counter[0], HIST)
    row = iota((HIST, 128), 0)
    lane = iota((HIST, 128), 1)
    low_lane = lane < HIST

    def unpacked(a):
        kept = jnp.where(iota((8, 128), 1) // HIST == iota((8, 128), 0), gram[4 + a : 5 + a, :], 0.0)
        for shift in (16, 32, 64):
            kept = kept + pltpu.roll(kept, shift, 1)
        return kept

    sy = jnp.where(low_lane, jnp.concatenate([unpacked(0), unpacked(1)], axis=0), 0.0)
    yy = jnp.where(low_lane, jnp.concatenate([unpacked(2), unpacked(3)], axis=0), 0.0)
    diag = row == lane
    is_new = jnp.logical_and(diag, row == newest)
    pick = lambda m: jnp.sum(jnp.sum(jnp.where(is_new, m, 0.0), axis=0, keepdims=True), axis=1, keepdims=True)
    gamma = pick(sy) / pick(yy)
    rank = lax.rem(newest - row + HIST, HIST)
    curv = jnp.sum(jnp.where(diag, sy, 0.0), axis=1, keepdims=True)
    rho = 1.0 / curv
    inv = diag.astype(f32)
    for step in range(HIST):
        here = row == lax.rem(newest - step + HIST, HIST)
        there = lane == lax.rem(newest - step + HIST, HIST)
        line = jnp.sum(jnp.where(here, inv * rho, 0.0), axis=0, keepdims=True)
        column = jnp.sum(jnp.where(there, sy, 0.0), axis=1, keepdims=True)
        later = inv - column * line
        inv = jnp.where(here, jnp.broadcast_to(line, inv.shape), jnp.where(rank > step, later, inv))
    pad = jnp.zeros((128 - HIST, 128), f32)
    inv_t = jnp.concatenate([inv, pad], axis=0).T[:HIST]
    middle = gamma * yy + jnp.where(diag, sy, 0.0)
    inner = jnp.dot(middle, jnp.concatenate([inv, pad], axis=0), precision=highest, preferred_element_type=f32)
    corner = jnp.dot(inv_t, jnp.concatenate([inner, pad], axis=0), precision=highest, preferred_element_type=f32)
    out[0:HIST, :] = corner - gamma * pltpu.roll(inv_t, HIST, 1)
    out[HIST : 2 * HIST, :] = -gamma * inv
    out[2 * HIST :, :] = jnp.broadcast_to(gamma, (8, 128))


def last_kernel(crosses, solve, total, wrow, hist, new_weights, gradient):
    line = jnp.sum(crosses[...], axis=0)
    coefs = jnp.sum(solve[0 : 2 * HIST, :] * line, axis=1, keepdims=True)
    gamma = solve[2 * HIST : 2 * HIST + 1, 0:1]
    weights = wrow[...]
    grad = weights + penalty * total[...]
    gradient[...] = grad
    mixed = jnp.sum(hist[...] * coefs, axis=0, keepdims=True)
    new_weights[...] = weights - step_length * (gamma * grad + mixed)


def swapped(array, mask):
    count = lax.axis_size(ROWS)
    return array + lax.ppermute(array, ROWS, [(i, i ^ mask) for i in range(count)])


SMALL = pltpu.CompilerParams(vmem_limit_bytes=16 * 1024 * 1024)
VM = pl.BlockSpec(memory_space=pltpu.VMEM)
HB = pl.BlockSpec(memory_space=pltpu.HBM)


def body(samples, labels, weights, hist_s, hist_y, counter):
    count, feats = samples.shape
    samp, hist, wrow, part = pl.pallas_call(
        first_kernel,
        in_specs=[HB, HB, HB, HB],
        out_specs=[VM, VM, VM, VM],
        out_shape=[
            pltpu.VMEM((count, feats), bf16),
            pltpu.VMEM((2 * HIST, feats), f32),
            pltpu.VMEM((1, feats), f32),
            pltpu.VMEM((16, 8, 128), f32),
        ],
        scratch_shapes=[pltpu.SemaphoreType.DMA((3 + CHUNKS,))],
        compiler_params=SMALL,
        name="first",
    )(samples, weights.reshape(1, feats), hist_s, hist_y)
    parts = lax.all_to_all(part, COLS, split_axis=0, concat_axis=0, tiled=True)
    total, cross, gram = pl.pallas_call(
        second_kernel,
        in_specs=[VM] * 5,
        out_specs=[VM] * 3,
        out_shape=[
            pltpu.VMEM((1, feats), f32),
            pltpu.VMEM((128, 1, 128), f32),
            pltpu.VMEM((8, 128), f32),
        ],
        compiler_params=SMALL,
        name="second",
    )(parts, labels.reshape(1, count), samp, hist, wrow)
    crosses = lax.all_to_all(cross, (ROWS, COLS), split_axis=0, concat_axis=0, tiled=True)
    for mask in (7, 3, 1):
        total = swapped(total, mask)
    solve = pl.pallas_call(
        solve_kernel,
        in_specs=[pl.BlockSpec(memory_space=pltpu.SMEM), VM],
        out_specs=VM,
        out_shape=pltpu.VMEM((40, 128), f32),
        compiler_params=SMALL,
        name="solve",
    )(counter, gram)
    new_weights, gradient = pl.pallas_call(
        last_kernel,
        in_specs=[VM] * 5,
        out_specs=[VM] * 2,
        out_shape=[jax.ShapeDtypeStruct((1, feats), f32)] * 2,
        compiler_params=SMALL,
        name="last",
    )(crosses, solve, total, wrow, hist)
    return new_weights.reshape(feats), gradient.reshape(feats)


def solution(mesh):
    return jax.shard_map(
        body,
        mesh=mesh,
        in_specs=(P(ROWS, COLS), P(ROWS), P(COLS), P(None, COLS), P(None, COLS), P()),
        out_specs=(P(COLS), P(COLS)),
        check_vma=False,
    )
```

time: 130 us -> 45.8 us (0.35)
  matrix products: 44.6 us -> 0 us
  between operations: 34.9 us -> 1.34 us
  waiting for transfers between devices: 15.1 us -> 5.36 us
  starting transfers between devices: 20.5 us -> 11 us
  Pallas kernels: 0 us -> 8.01 us
  blocking collectives: 9.32 us -> 14.9 us
  local copies, waits for them, and re-layouts: 2.35 us -> 4.8 us
  other arithmetic: 2.35 us -> 0.07 us
    dot_general x54 -> x0, matrix products: 44.6 us -> none  [the longest x49 37.2 us: quad_form(): jnp.dot(matrix, right, precision=highest)]
    all_to_all x3 -> x1, waiting for transfers between devices: 15.1 us -> 0.01 us  [body(): lax.all_to_all(cross, (ROWS, COLS), split_axis=0, concat_axis=0, tiled=True)]
    all_to_all x3 -> x1, starting transfers between devices: 20.5 us -> 7.38 us  [body(): lax.all_to_all(cross, (ROWS, COLS), split_axis=0, concat_axis=0, tiled=True)]
    pallas_call x0 -> x4, Pallas kernels: none -> 8.01 us  [the longest x1 4.85 us: body(): pl.pallas_call(first_kernel, in_specs=[HB, HB, HB, HB], out_specs=[VM, VM...]
    all_to_all x1, blocking collectives: 9.32 us -> 14.9 us  [body(): parts = lax.all_to_all(part, COLS, split_axis=0, concat_axis=0, tiled=True)]
    ppermute x0 -> x3, waiting for transfers between devices: none -> 5.35 us  [swapped(): lax.ppermute(array, ROWS, [(i, i ^ mask) for i in range(count)])]
    unnamed x11 -> x10, local copies, waits for them, and re-layouts: 0.05 us -> 4.8 us
    ppermute x0 -> x3, starting transfers between devices: none -> 3.64 us  [swapped(): lax.ppermute(array, ROWS, [(i, i ^ mask) for i in range(count)])]
  transfers between devices with their start and end apart: 3 -> 4, of which waited for: 3 -> 2; matrix products, arithmetic and copies ran while one was open for 0% -> 0% of each run, Pallas kernels for 0% -> 2%
where the time goes in v1:
time: 45.8 us; the launch traced here: 45.5 us
  blocking collectives  14.9 us (33%)
  starting transfers between devices  11 us (24%)
  Pallas kernels  8.01 us (17%)
  waiting for transfers between devices  5.36 us (12%)
  local copies, waits for them, and re-layouts  4.8 us (10%)
  between operations  1.34 us (3%)
    all_to_all x1, blocking collectives, body(): parts = lax.all_to_all(part, COLS, split_axis=0, concat_axis=0, tiled=True)  14.9 us
    all_to_all x1, starting transfers between devices, body(): lax.all_to_all(cross, (ROWS, COLS), split_axis=0, concat_axis=0, tiled=True)  7.38 us
    ppermute x3, waiting for transfers between devices, swapped(): lax.ppermute(array, ROWS, [(i, i ^ mask) for i in range(count)])  5.35 us
    pallas_call x1, Pallas kernels, body(): pl.pallas_call(first_kernel, in_specs=[HB, HB, HB, HB], out_specs=[VM, VM...  4.85 us
    unnamed x10, local copies, waits for them, and re-layouts  4.8 us
    ppermute x3, starting transfers between devices, swapped(): lax.ppermute(array, ROWS, [(i, i ^ mask) for i in range(count)])  3.64 us
    pallas_call x1, Pallas kernels, body(): pl.pallas_call(second_kernel, in_specs=[VM] * 5, out_specs=[VM] * 3, out_...  1.45 us
  transfers between devices with their start and end apart: 4, of which 2 were waited for; matrix products, arithmetic and copies ran while one was open for 0% of the time, Pallas kernels for 2%

profile of v1, /device:TPU:1, one launch (start us, length us, event | category | flops | bytes accessed | tf_op | source)
XLA Modules:
  0.0 45.5 jit_solution(17020443336085782646)
XLA Ops:
  0.6 0.0 copy-start
  0.6 2.2 %copy-done = bf16[512,4096]{1,0:T(8,128)(2,1)S(1)} copy-done((bf16[512,4096]{1,0:T(8,128)(2,1)S(1)}, bf16[512,4096]{1,0:T(8,128)(2,1)}, u32[]{:S(2)}) %copy-start) | copy-done | bytes 4194328
  2.8 0.0 copy-start.1
  2.8 0.9 %copy-done.1 = f32[16,4096]{1,0:T(8,128)S(1)} copy-done((f32[16,4096]{1,0:T(8,128)S(1)}, f32[16,4096]{1,0:T(8,128)}, u32[]{:S(2)}) %copy-start.1) | copy-done | bytes 262168
  3.8 0.0 copy-start.2
  3.8 0.9 %copy-done.2 = f32[16,4096]{1,0:T(8,128)S(1)} copy-done((f32[16,4096]{1,0:T(8,128)S(1)}, f32[16,4096]{1,0:T(8,128)}, u32[]{:S(2)}) %copy-start.2) | copy-done | bytes 262168
  4.7 0.0 copy-start.3
  4.7 0.7 %copy-done.3 = f32[4096]{0:T(1024)S(1)} copy-done((f32[4096]{0:T(1024)S(1)}, f32[4096]{0:T(1024)}, u32[]{:S(2)}) %copy-start.3) | copy-done | bytes 16408
  5.4 0.0 copy-start.4
  5.4 4.9 %first.1 = (bf16[512,4096]{1,0:T(8,128)(2,1)S(1)}, f32[32,4096]{1,0:T(8,128)S(1)}, f32[1,4096]{1,0:T(1,128)S(1)}, f32[16,8,128]{2,1,0:T(8,128)S(1)}) custom-call(bf16[512,4096]{1,0:T(8,128)(2,1)S(1)} %copy-done, f32[1,4096]{1,0:T(1,128)S(1)} %bitcast.4, f32[16,4096]{1,0:T(8,128)S(1)} %copy-done.1, f32[16,4096]{1,0:T(8,128)S(1)} %copy-done.2), custom_call_target="tpu_custom_call" | custom-call | tf_op jit(solution)/shard_map/first/pallas_call | solution.py:151
  10.3 14.9 %all_to_all.10.parts = f32[16,8,128]{2,1,0:T(8,128)S(1)} all-to-all(f32[16,8,128]{2,1,0:T(8,128)S(1)} %get-tuple-element.11), channel_id=1, replica_groups=mesh['rows'=8,'cols'=16] {'cols'}, dimensions={0} | all-to-all | bytes 131072 | tf_op jit(solution)/shard_map/all_to_all | solution.py:165
  25.2 0.0 copy-done.4
  25.2 1.4 %second.1 = (f32[1,4096]{1,0:T(1,128)S(1)}, f32[128,1,128]{2,1,0:T(1,128)}, f32[8,128]{1,0:T(8,128)S(1)}) custom-call(f32[16,8,128]{2,1,0:T(8,128)S(1)} %all_to_all.10.parts, s32[1,512]{1,0:T(1,128)S(1)} %bitcast.5, bf16[512,4096]{1,0:T(8,128)(2,1)S(1)} %get-tuple-element.12.samp, f32[32,4096]{1,0:T(8,128)S(1)} %get-tuple-element.13.hist, ...), custom_call_target="tpu_custom_call" | custom-call | tf_op jit(solution)/shard_map/second/pallas_call | solution.py:166
  26.7 7.4 %all-to-all-start.1 = ((f32[128,1,128]{2,1,0:T(1,128)}), f32[128,1,128]{2,1,0:T(1,128)S(1)}, u32[]{:S(2)}, u32[]{:S(2)}) async-start(f32[128,1,128]{2,1,0:T(1,128)} %get-tuple-element.15), calls=%async_computation.1 | async-start | bytes 131072 | tf_op jit(solution)/shard_map/all_to_all | solution.py:178
  34.0 2.9 %collective-permute-start = (f32[1,4096]{1,0:T(1,128)S(1)}, f32[1,4096]{1,0:T(1,128)S(1)}, u32[]{:S(2)}, u32[]{:S(2)}) collective-permute-start(f32[1,4096]{1,0:T(1,128)S(1)} %get-tuple-element.17), channel_id=1, source_target_pairs={{0,112},{16,96},{32,80},{48,64},{64,48},{80,32},{96,16},{112,0},{1... | collective-permute-start | bytes 49160 | tf_op jit(solution)/shard_map/ppermute | solution.py:141
  37.0 1.9 %collective-permute-done = f32[1,4096]{1,0:T(1,128)S(1)} collective-permute-done((f32[1,4096]{1,0:T(1,128)S(1)}, f32[1,4096]{1,0:T(1,128)S(1)}, u32[]{:S(2)}, u32[]{:S(2)}) %collective-permute-start) | collective-permute-done | bytes 16416 | tf_op jit(solution)/shard_map/ppermute | solution.py:141
  38.9 0.2 collective-permute-start.1
  39.1 3.5 %collective-permute-done.1 = f32[1,4096]{1,0:T(1,128)S(1)} collective-permute-done((f32[1,4096]{1,0:T(1,128)S(1)}, f32[1,4096]{1,0:T(1,128)S(1)}, u32[]{:S(2)}, u32[]{:S(2)}) %collective-permute-start.1) | collective-permute-done | bytes 16416 | tf_op jit(solution)/shard_map/ppermute | solution.py:141
  42.6 0.5 %collective-permute-start.2 = (f32[1,4096]{1,0:T(1,128)S(1)}, f32[1,4096]{1,0:T(1,128)S(1)}, u32[]{:S(2)}, u32[]{:S(2)}) collective-permute-start(f32[1,4096]{1,0:T(1,128)S(1)} %add.10), channel_id=1, source_target_pairs={{0,16},{16,0},{32,48},{48,32},{64,80},{80,64},{96,112},{112,96},{1... | collective-permute-start | bytes 49160 | tf_op jit(solution)/shard_map/ppermute | solution.py:141
  43.7 0.8 %solve.1 = f32[40,128]{1,0:T(8,128)S(1)} custom-call(s32[1]{0:T(128)S(6)} %copy.8.counter, f32[8,128]{1,0:T(8,128)S(1)} %get-tuple-element.16.gram), custom_call_target="tpu_custom_call" | custom-call | tf_op jit(solution)/shard_map/solve/pallas_call | solution.py:181
  44.5 0.0 collective-permute-done.2
  44.6 0.0 all-to-all-done.1.crosses
  44.6 0.9 %last.1 = (f32[1,4096]{1,0:T(1,128)}, f32[1,4096]{1,0:T(1,128)}) custom-call(f32[128,1,128]{2,1,0:T(1,128)S(1)} %all-to-all-done.1.crosses, f32[40,128]{1,0:T(8,128)S(1)} %solve.1, f32[1,4096]{1,0:T(1,128)S(1)} %add.11.total, f32[1,4096]{1,0:T(1,128)S(1)} %get-tuple-element.14.wrow, f32[32,4096]{1,0:T(8,128)S(1)} %get-tuple-element.13.hist), custom_call_target="tpu_custom_call" | custom-call | tf_op jit(solution)/shard_map/last/pallas_call | solution.py:189
  (3 shorter events, 0.1 us)
Async XLA Ops:
  0.6 2.2 %copy-start = (bf16[512,4096]{1,0:T(8,128)(2,1)S(1)}, bf16[512,4096]{1,0:T(8,128)(2,1)}, u32[]{:S(2)}) copy-start(bf16[512,4096]{1,0:T(8,128)(2,1)} %s_hbm.1) | copy-start | bytes 12582916
  2.8 0.9 %copy-start.1 = (f32[16,4096]{1,0:T(8,128)S(1)}, f32[16,4096]{1,0:T(8,128)}, u32[]{:S(2)}) copy-start(f32[16,4096]{1,0:T(8,128)} %hs_hbm.1) | copy-start | bytes 786436
  3.8 0.9 %copy-start.2 = (f32[16,4096]{1,0:T(8,128)S(1)}, f32[16,4096]{1,0:T(8,128)}, u32[]{:S(2)}) copy-start(f32[16,4096]{1,0:T(8,128)} %hy_hbm.1) | copy-start | bytes 786436
  4.7 0.7 %copy-start.3 = (f32[4096]{0:T(1024)S(1)}, f32[4096]{0:T(1024)}, u32[]{:S(2)}) copy-start(f32[4096]{0:T(1024)} %param.8) | copy-start | bytes 49156
  5.4 19.8 %copy-start.4 = (s32[512]{0:T(512)S(1)}, s32[512]{0:T(512)}, u32[]{:S(2)}) copy-start(s32[512]{0:T(512)} %param.7) | copy-start | bytes 6148
  26.7 17.9 %all-to-all-start.1 = ((f32[128,1,128]{2,1,0:T(1,128)}), f32[128,1,128]{2,1,0:T(1,128)S(1)}, u32[]{:S(2)}, u32[]{:S(2)}) async-start(f32[128,1,128]{2,1,0:T(1,128)} %get-tuple-element.15), calls=%async_computation.1 | async-start | bytes 131072 | tf_op jit(solution)/shard_map/all_to_all | solution.py:178
  34.0 4.8 %collective-permute-start = (f32[1,4096]{1,0:T(1,128)S(1)}, f32[1,4096]{1,0:T(1,128)S(1)}, u32[]{:S(2)}, u32[]{:S(2)}) collective-permute-start(f32[1,4096]{1,0:T(1,128)S(1)} %get-tuple-element.17), channel_id=1, source_target_pairs={{0,112},{16,96},{32,80},{48,64},{64,48},{80,32},{96,16},{112,0},{1... | collective-permute-start | bytes 49160 | tf_op jit(solution)/shard_map/ppermute | solution.py:141
  38.9 3.7 %collective-permute-start.1 = (f32[1,4096]{1,0:T(1,128)S(1)}, f32[1,4096]{1,0:T(1,128)S(1)}, u32[]{:S(2)}, u32[]{:S(2)}) collective-permute-start(f32[1,4096]{1,0:T(1,128)S(1)} %add.9), channel_id=1, source_target_pairs={{0,48},{16,32},{32,16},{48,0},{64,112},{80,96},{96,80},{112,64},{1... | collective-permute-start | bytes 49160 | tf_op jit(solution)/shard_map/ppermute | solution.py:141
  42.6 2.0 %collective-permute-start.2 = (f32[1,4096]{1,0:T(1,128)S(1)}, f32[1,4096]{1,0:T(1,128)S(1)}, u32[]{:S(2)}, u32[]{:S(2)}) collective-permute-start(f32[1,4096]{1,0:T(1,128)S(1)} %add.10), channel_id=1, source_target_pairs={{0,16},{16,0},{32,48},{48,32},{64,80},{80,64},{96,112},{112,96},{1... | collective-permute-start | bytes 49160 | tf_op jit(solution)/shard_map/ppermute | solution.py:141

commit v2 on v1

--- a/solution.py
+++ b/solution.py
@@ -161,7 +161,7 @@
         scratch_shapes=[pltpu.SemaphoreType.DMA((3 + CHUNKS,))],
         compiler_params=SMALL,
         name="first",
-    )(samples, weights.reshape(1, feats), hist_s, hist_y)
+    )(*(pltpu.with_memory_space_constraint(a, pltpu.HBM) for a in (samples, weights.reshape(1, feats), hist_s, hist_y)))
     parts = lax.all_to_all(part, COLS, split_axis=0, concat_axis=0, tiled=True)
     total, cross, gram = pl.pallas_call(
         second_kernel,

time: 45.8 us -> 40.8 us (0.89)
  local copies, waits for them, and re-layouts: 4.8 us -> 0.01 us
    unnamed x10 -> x2, local copies, waits for them, and re-layouts: 4.8 us -> 0.01 us
where the time goes in v2:
time: 40.8 us; the launch traced here: 40.7 us
  blocking collectives  14.9 us (37%)
  starting transfers between devices  11.1 us (27%)
  Pallas kernels  7.97 us (20%)
  waiting for transfers between devices  5.3 us (13%)
  between operations  1.33 us (3%)
    all_to_all x1, blocking collectives, body(): parts = lax.all_to_all(part, COLS, split_axis=0, concat_axis=0, tiled=True)  14.9 us
    all_to_all x1, starting transfers between devices, body(): lax.all_to_all(cross, (ROWS, COLS), split_axis=0, concat_axis=0, tiled=True)  7.38 us
    ppermute x3, waiting for transfers between devices, swapped(): lax.ppermute(array, ROWS, [(i, i ^ mask) for i in range(count)])  5.29 us
    pallas_call x1, Pallas kernels, body(): pl.pallas_call(first_kernel, in_specs=[HB, HB, HB, HB], out_specs=[VM, VM...  4.82 us
    ppermute x3, starting transfers between devices, swapped(): lax.ppermute(array, ROWS, [(i, i ^ mask) for i in range(count)])  3.69 us
    pallas_call x1, Pallas kernels, body(): pl.pallas_call(second_kernel, in_specs=[VM] * 5, out_specs=[VM] * 3, out_...  1.45 us
    pallas_call x1, Pallas kernels, body(): pl.pallas_call(last_kernel, in_specs=[VM] * 5, out_specs=[VM] * 2, out_sh...  0.91 us
  transfers between devices with their start and end apart: 4, of which 2 were waited for; matrix products, arithmetic and copies ran while one was open for 0% of the time, Pallas kernels for 2%

profile of v2, /device:TPU:1, one launch (start us, length us, event | category | flops | bytes accessed | tf_op | source)
XLA Modules:
  0.0 40.7 jit_solution(14627860477047648274)
XLA Ops:
  0.6 0.0 copy-start
  0.6 4.8 %first.1 = (bf16[512,4096]{1,0:T(8,128)(2,1)S(1)}, f32[32,4096]{1,0:T(8,128)S(1)}, f32[1,4096]{1,0:T(1,128)S(1)}, f32[16,8,128]{2,1,0:T(8,128)S(1)}) custom-call(bf16[512,4096]{1,0:T(8,128)(2,1)} %s_hbm.1, f32[1,4096]{1,0:T(1,128)} %bitcast.5, f32[16,4096]{1,0:T(8,128)} %hs_hbm.1, f32[16,4096]{1,0:T(8,128)} %hy_hbm.1), custom_call_target="tpu_custom_call" | custom-call | tf_op jit(solution)/shard_map/first/pallas_call | solution.py:151
  5.5 14.9 %all_to_all.10.parts = f32[16,8,128]{2,1,0:T(8,128)S(1)} all-to-all(f32[16,8,128]{2,1,0:T(8,128)S(1)} %get-tuple-element.11), channel_id=1, replica_groups=mesh['rows'=8,'cols'=16] {'cols'}, dimensions={0} | all-to-all | bytes 131072 | tf_op jit(solution)/shard_map/all_to_all | solution.py:165
  20.4 0.0 copy-done
  20.4 1.4 %second.1 = (f32[1,4096]{1,0:T(1,128)S(1)}, f32[128,1,128]{2,1,0:T(1,128)}, f32[8,128]{1,0:T(8,128)S(1)}) custom-call(f32[16,8,128]{2,1,0:T(8,128)S(1)} %all_to_all.10.parts, s32[1,512]{1,0:T(1,128)S(1)} %bitcast.4, bf16[512,4096]{1,0:T(8,128)(2,1)S(1)} %get-tuple-element.12.samp, f32[32,4096]{1,0:T(8,128)S(1)} %get-tuple-element.13.hist, ...), custom_call_target="tpu_custom_call" | custom-call | tf_op jit(solution)/shard_map/second/pallas_call | solution.py:166
  21.8 7.4 %all-to-all-start.1 = ((f32[128,1,128]{2,1,0:T(1,128)}), f32[128,1,128]{2,1,0:T(1,128)S(1)}, u32[]{:S(2)}, u32[]{:S(2)}) async-start(f32[128,1,128]{2,1,0:T(1,128)} %get-tuple-element.15), calls=%async_computation.1 | async-start | bytes 131072 | tf_op jit(solution)/shard_map/all_to_all | solution.py:178
  29.2 2.9 %collective-permute-start = (f32[1,4096]{1,0:T(1,128)S(1)}, f32[1,4096]{1,0:T(1,128)S(1)}, u32[]{:S(2)}, u32[]{:S(2)}) collective-permute-start(f32[1,4096]{1,0:T(1,128)S(1)} %get-tuple-element.17), channel_id=1, source_target_pairs={{0,112},{16,96},{32,80},{48,64},{64,48},{80,32},{96,16},{112,0},{1... | collective-permute-start | bytes 49160 | tf_op jit(solution)/shard_map/ppermute | solution.py:141
  32.1 1.9 %collective-permute-done = f32[1,4096]{1,0:T(1,128)S(1)} collective-permute-done((f32[1,4096]{1,0:T(1,128)S(1)}, f32[1,4096]{1,0:T(1,128)S(1)}, u32[]{:S(2)}, u32[]{:S(2)}) %collective-permute-start) | collective-permute-done | bytes 16416 | tf_op jit(solution)/shard_map/ppermute | solution.py:141
  34.0 0.3 collective-permute-start.1
  34.3 3.4 %collective-permute-done.1 = f32[1,4096]{1,0:T(1,128)S(1)} collective-permute-done((f32[1,4096]{1,0:T(1,128)S(1)}, f32[1,4096]{1,0:T(1,128)S(1)}, u32[]{:S(2)}, u32[]{:S(2)}) %collective-permute-start.1) | collective-permute-done | bytes 16416 | tf_op jit(solution)/shard_map/ppermute | solution.py:141
  37.7 0.5 %collective-permute-start.2 = (f32[1,4096]{1,0:T(1,128)S(1)}, f32[1,4096]{1,0:T(1,128)S(1)}, u32[]{:S(2)}, u32[]{:S(2)}) collective-permute-start(f32[1,4096]{1,0:T(1,128)S(1)} %add.10), channel_id=1, source_target_pairs={{0,16},{16,0},{32,48},{48,32},{64,80},{80,64},{96,112},{112,96},{1... | collective-permute-start | bytes 49160 | tf_op jit(solution)/shard_map/ppermute | solution.py:141
  38.9 0.8 %solve.1 = f32[40,128]{1,0:T(8,128)S(1)} custom-call(s32[1]{0:T(128)S(6)} %copy.8.counter, f32[8,128]{1,0:T(8,128)S(1)} %get-tuple-element.16.gram), custom_call_target="tpu_custom_call" | custom-call | tf_op jit(solution)/shard_map/solve/pallas_call | solution.py:181
  39.7 0.0 collective-permute-done.2
  39.7 0.0 all-to-all-done.1.crosses
  39.7 0.9 %last.1 = (f32[1,4096]{1,0:T(1,128)}, f32[1,4096]{1,0:T(1,128)}) custom-call(f32[128,1,128]{2,1,0:T(1,128)S(1)} %all-to-all-done.1.crosses, f32[40,128]{1,0:T(8,128)S(1)} %solve.1, f32[1,4096]{1,0:T(1,128)S(1)} %add.11.total, f32[1,4096]{1,0:T(1,128)S(1)} %get-tuple-element.14.wrow, f32[32,4096]{1,0:T(8,128)S(1)} %get-tuple-element.13.hist), custom_call_target="tpu_custom_call" | custom-call | tf_op jit(solution)/shard_map/last/pallas_call | solution.py:189
  (3 shorter events, 0.1 us)
Async XLA Ops:
  0.6 19.7 %copy-start = (s32[512]{0:T(512)S(1)}, s32[512]{0:T(512)}, u32[]{:S(2)}) copy-start(s32[512]{0:T(512)} %param.7) | copy-start | bytes 6148
  21.8 17.9 %all-to-all-start.1 = ((f32[128,1,128]{2,1,0:T(1,128)}), f32[128,1,128]{2,1,0:T(1,128)S(1)}, u32[]{:S(2)}, u32[]{:S(2)}) async-start(f32[128,1,128]{2,1,0:T(1,128)} %get-tuple-element.15), calls=%async_computation.1 | async-start | bytes 131072 | tf_op jit(solution)/shard_map/all_to_all | solution.py:178
  29.2 4.8 %collective-permute-start = (f32[1,4096]{1,0:T(1,128)S(1)}, f32[1,4096]{1,0:T(1,128)S(1)}, u32[]{:S(2)}, u32[]{:S(2)}) collective-permute-start(f32[1,4096]{1,0:T(1,128)S(1)} %get-tuple-element.17), channel_id=1, source_target_pairs={{0,112},{16,96},{32,80},{48,64},{64,48},{80,32},{96,16},{112,0},{1... | collective-permute-start | bytes 49160 | tf_op jit(solution)/shard_map/ppermute | solution.py:141
  34.0 3.7 %collective-permute-start.1 = (f32[1,4096]{1,0:T(1,128)S(1)}, f32[1,4096]{1,0:T(1,128)S(1)}, u32[]{:S(2)}, u32[]{:S(2)}) collective-permute-start(f32[1,4096]{1,0:T(1,128)S(1)} %add.9), channel_id=1, source_target_pairs={{0,48},{16,32},{32,16},{48,0},{64,112},{80,96},{96,80},{112,64},{1... | collective-permute-start | bytes 49160 | tf_op jit(solution)/shard_map/ppermute | solution.py:141
  37.7 2.0 %collective-permute-start.2 = (f32[1,4096]{1,0:T(1,128)S(1)}, f32[1,4096]{1,0:T(1,128)S(1)}, u32[]{:S(2)}, u32[]{:S(2)}) collective-permute-start(f32[1,4096]{1,0:T(1,128)S(1)} %add.10), channel_id=1, source_target_pairs={{0,16},{16,0},{32,48},{48,32},{64,80},{80,64},{96,112},{112,96},{1... | collective-permute-start | bytes 49160 | tf_op jit(solution)/shard_map/ppermute | solution.py:141

commit v3 on v2

--- a/solution.py
+++ b/solution.py
@@ -5,6 +5,7 @@
 from jax.experimental.pallas import tpu as pltpu
 from jax.sharding import PartitionSpec as P
 
+
 HIST = 16
 ROWS = "rows"
 COLS = "cols"
@@ -25,8 +26,9 @@
     return lax.dot_general(left, right, (((1,), (1,)), ((), ())), preferred_element_type=f32)
 
 
-def first_kernel(s_hbm, w_hbm, hs_hbm, hy_hbm, samp, hist, wrow, part, sems):
+def first_kernel(s_hbm, w_hbm, hs_hbm, hy_hbm, samp, hist, wrow, part, proj, bias, sems):
     feats = samp.shape[1]
+    count = samp.shape[0]
     width = feats // CHUNKS
     copies = [
         pltpu.make_async_copy(hs_hbm, hist.at[pl.ds(0, HIST), :], sems.at[0]),
@@ -40,50 +42,54 @@
         copy.start()
     for copy in copies[:3]:
         copy.wait()
-    h = hist[...]
-    high = h.astype(bf16)
-    low = (h - high.astype(f32)).astype(bf16)
-    y_high = high[HIST:]
-    y_low = low[HIST:]
-    right = jnp.concatenate([y_high] * 8 + [y_low] * 8, axis=0)
-    left = jnp.concatenate([high, low], axis=0)
-    both = dot_t(left, right)
-    gram = (both[:32, 128:] + both[32:, :128]) + both[:32, :128]
-    mask = iota((32, 128), 1) // HIST == iota((32, 128), 0) % 8
-    gram = jnp.where(mask, gram, 0.0)
-    packed = [jnp.sum(gram[8 * a : 8 * a + 8], axis=0, keepdims=True) for a in range(4)]
-
-    acc = jnp.zeros((16, samp.shape[0]), f32)
+    acc = jnp.zeros((16 + 4 * HIST, count), f32)
+    both = jnp.zeros((4 * HIST, 48), f32)
     for c in range(CHUNKS):
         copies[3 + c].wait()
         cols = slice(c * width, (c + 1) * width)
-        w16 = jnp.broadcast_to(wrow[:, cols].astype(bf16), (16, width))
-        acc = acc + dot_t(w16, samp[:, cols])
+        h = hist[:, cols]
+        high = h.astype(bf16)
+        low = (h - high.astype(f32)).astype(bf16)
+        w = wrow[:, cols]
+        w16 = w.astype(bf16)
+        w_low = (w - w16.astype(f32)).astype(bf16)
+        w_pair = jnp.where(iota((16, width), 0) == 0, w16.astype(f32), w_low.astype(f32)).astype(bf16)
+        right = jnp.concatenate([high[HIST:], low[HIST:], w_pair], axis=0)
+        left = jnp.concatenate([jnp.broadcast_to(w16, (16, width)), high, low], axis=0)
+        acc = acc + dot_t(left, samp[:, cols])
+        both = both + dot_t(left[16:], right)
+    proj[...] = penalty * (acc[16 : 16 + 2 * HIST] + acc[16 + 2 * HIST :])
+    both = jnp.concatenate([both, jnp.zeros((4 * HIST, 80), f32)], axis=1)
+    halves = both[: 2 * HIST] + both[2 * HIST :]
+    lane = iota((2 * HIST, 128), 1)
+    bias[...] = jnp.where(jnp.logical_or(lane == 32, lane == 33), 0.125 * halves, 0.0)
+    gram = jnp.where(lane < HIST, halves + pltpu.roll(halves, 128 - HIST, 1), 0.0)
+    for shift in (16, 32, 64):
+        gram = gram + pltpu.roll(gram, shift, 1)
+    gram = jnp.where(lane // HIST == iota((2 * HIST, 128), 0) % 8, gram, 0.0)
+    packed = [jnp.sum(gram[8 * a : 8 * a + 8], axis=0, keepdims=True) for a in range(4)]
     rows = [acc[0:1, 128 * i : 128 * i + 128] for i in range(4)]
     mine = jnp.concatenate(rows + packed, axis=0)
     part[...] = jnp.broadcast_to(mine[None], part.shape)
 
 
-def second_kernel(parts, labels, samp, hist, wrow, total, cross, gram):
+def second_kernel(parts, labels, proj, bias, samp, cross_hbm, gram, total, cross, sem):
     summed = jnp.sum(parts[...], axis=0)
     gram[...] = summed
     margin = jnp.concatenate([summed[i : i + 1] for i in range(4)], axis=1)
     resid = (jax.nn.sigmoid(margin) - labels[...].astype(f32)).astype(bf16)
-    resid16 = jnp.broadcast_to(resid, (16, resid.shape[1]))
-    feats = samp.shape[1]
-    width = 512
-    acc = jnp.zeros((2 * HIST, 128), f32)
-    for c in range(feats // width):
-        cols = slice(c * width, (c + 1) * width)
-        t = jnp.dot(resid16, samp[:, cols], preferred_element_type=f32)[0:1]
-        total[:, cols] = t
-        lead = wrow[:, cols] * 0.125 + penalty * t
-        prod = hist[:, cols] * lead
-        for k in range(width // 128):
-            acc = acc + prod[:, 128 * k : 128 * k + 128]
+    prod = proj[...] * resid.astype(f32)
+    acc = bias[...]
+    for i in range(4):
+        acc = acc + prod[:, 128 * i : 128 * i + 128]
     square = jnp.concatenate([acc, jnp.zeros((96, 128), f32)], axis=0)
     line = jnp.sum(square.T, axis=0, keepdims=True)
     cross[...] = jnp.broadcast_to(line[None], cross.shape)
+    out = pltpu.make_async_copy(cross, cross_hbm, sem)
+    out.start()
+    resid16 = jnp.broadcast_to(resid, (16, resid.shape[1]))
+    total[...] = jnp.dot(resid16, samp[...], preferred_element_type=f32)[0:1]
+    out.wait()
 
 
 def solve_kernel(counter, gram, out):
@@ -125,20 +131,22 @@
     out[2 * HIST :, :] = jnp.broadcast_to(gamma, (8, 128))
 
 
-def last_kernel(crosses, solve, total, wrow, hist, new_weights, gradient):
+def gradient_kernel(mine, other, solve, wrow, gradient, base):
+    weights = wrow[...]
+    grad = weights + penalty * (mine[...] + other[...])
+    gradient[...] = grad
+    base[...] = weights - (step_length * solve[2 * HIST : 2 * HIST + 1, 0:1]) * grad
+
+
+def last_kernel(crosses, solve, base, hist, new_weights):
     line = jnp.sum(crosses[...], axis=0)
-    coefs = jnp.sum(solve[0 : 2 * HIST, :] * line, axis=1, keepdims=True)
-    gamma = solve[2 * HIST : 2 * HIST + 1, 0:1]
-    weights = wrow[...]
-    grad = weights + penalty * total[...]
-    gradient[...] = grad
-    mixed = jnp.sum(hist[...] * coefs, axis=0, keepdims=True)
-    new_weights[...] = weights - step_length * (gamma * grad + mixed)
+    coefs = step_length * jnp.sum(solve[0 : 2 * HIST, :] * line, axis=1, keepdims=True)
+    new_weights[...] = base[...] - jnp.sum(hist[...] * coefs, axis=0, keepdims=True)
 
 
 def swapped(array, mask):
     count = lax.axis_size(ROWS)
-    return array + lax.ppermute(array, ROWS, [(i, i ^ mask) for i in range(count)])
+    return lax.ppermute(array, ROWS, [(i, i ^ mask) for i in range(count)])
 
 
 SMALL = pltpu.CompilerParams(vmem_limit_bytes=16 * 1024 * 1024)
@@ -148,36 +156,42 @@
 
 def body(samples, labels, weights, hist_s, hist_y, counter):
     count, feats = samples.shape
-    samp, hist, wrow, part = pl.pallas_call(
+    samp, hist, wrow, part, proj, bias = pl.pallas_call(
         first_kernel,
-        in_specs=[HB, HB, HB, HB],
-        out_specs=[VM, VM, VM, VM],
+        in_specs=[HB] * 4,
+        out_specs=[VM] * 6,
         out_shape=[
             pltpu.VMEM((count, feats), bf16),
             pltpu.VMEM((2 * HIST, feats), f32),
             pltpu.VMEM((1, feats), f32),
             pltpu.VMEM((16, 8, 128), f32),
+            pltpu.VMEM((2 * HIST, count), f32),
+            pltpu.VMEM((2 * HIST, 128), f32),
         ],
         scratch_shapes=[pltpu.SemaphoreType.DMA((3 + CHUNKS,))],
         compiler_params=SMALL,
         name="first",
     )(*(pltpu.with_memory_space_constraint(a, pltpu.HBM) for a in (samples, weights.reshape(1, feats), hist_s, hist_y)))
     parts = lax.all_to_all(part, COLS, split_axis=0, concat_axis=0, tiled=True)
-    total, cross, gram = pl.pallas_call(
+    cross, gram, total = pl.pallas_call(
         second_kernel,
         in_specs=[VM] * 5,
-        out_specs=[VM] * 3,
+        out_specs=[HB, VM, VM],
         out_shape=[
+            jax.ShapeDtypeStruct((128, 1, 128), f32),
+            pltpu.VMEM((8, 128), f32),
             pltpu.VMEM((1, feats), f32),
-            pltpu.VMEM((128, 1, 128), f32),
-            pltpu.VMEM((8, 128), f32),
         ],
+        scratch_shapes=[pltpu.VMEM((128, 1, 128), f32), pltpu.SemaphoreType.DMA],
         compiler_params=SMALL,
         name="second",
-    )(parts, labels.reshape(1, count), samp, hist, wrow)
+    )(parts, labels.reshape(1, count), proj, bias, samp)
     crosses = lax.all_to_all(cross, (ROWS, COLS), split_axis=0, concat_axis=0, tiled=True)
-    for mask in (7, 3, 1):
-        total = swapped(total, mask)
+    other = swapped(total, 7)
+    total = total + other
+    other = swapped(total, 3)
+    total = total + other
+    other = swapped(total, 1)
     solve = pl.pallas_call(
         solve_kernel,
         in_specs=[pl.BlockSpec(memory_space=pltpu.SMEM), VM],
@@ -186,14 +200,22 @@
         compiler_params=SMALL,
         name="solve",
     )(counter, gram)
-    new_weights, gradient = pl.pallas_call(
+    gradient, base = pl.pallas_call(
+        gradient_kernel,
+        in_specs=[VM] * 4,
+        out_specs=[VM] * 2,
+        out_shape=[jax.ShapeDtypeStruct((1, feats), f32), pltpu.VMEM((1, feats), f32)],
+        compiler_params=SMALL,
+        name="gradient",
+    )(total, other, solve, wrow)
+    new_weights = pl.pallas_call(
         last_kernel,
-        in_specs=[VM] * 5,
-        out_specs=[VM] * 2,
-        out_shape=[jax.ShapeDtypeStruct((1, feats), f32)] * 2,
+        in_specs=[VM] * 4,
+        out_specs=VM,
+        out_shape=jax.ShapeDtypeStruct((1, feats), f32),
         compiler_params=SMALL,
         name="last",
-    )(crosses, solve, total, wrow, hist)
+    )(crosses, solve, base, hist)
     return new_weights.reshape(feats), gradient.reshape(feats)
 
 

time: 40.8 us -> 40 us (0.980)
  Pallas kernels: 7.97 us -> 7.18 us
    pallas_call x3 -> x4, Pallas kernels: 7.18 us -> 6.38 us  [the longest x1 3.6 us: body(): pl.pallas_call(first_kernel, in_specs=[HB] * 4, out_specs=[VM] * 6, out_s...]
  transfers between devices with their start and end apart: 4 -> 4, of which waited for: 2 -> 2; matrix products, arithmetic and copies ran while one was open for 0% -> 0% of each run, Pallas kernels for 2% -> 4%
where the time goes in v3:
time: 40 us; the launch traced here: 39.8 us
  blocking collectives  14.9 us (37%)
  starting transfers between devices  11.1 us (28%)
  Pallas kernels  7.18 us (18%)
  waiting for transfers between devices  5.3 us (13%)
  between operations  1.33 us (3%)
    all_to_all x1, blocking collectives, body(): parts = lax.all_to_all(part, COLS, split_axis=0, concat_axis=0, tiled=True)  14.9 us
    all_to_all x1, starting transfers between devices, body(): lax.all_to_all(cross, (ROWS, COLS), split_axis=0, concat_axis=0, tiled=True)  7.39 us
    ppermute x3, waiting for transfers between devices, swapped(): return lax.ppermute(array, ROWS, [(i, i ^ mask) for i in range(count)])  5.29 us
    ppermute x3, starting transfers between devices, swapped(): return lax.ppermute(array, ROWS, [(i, i ^ mask) for i in range(count)])  3.69 us
    pallas_call x1, Pallas kernels, body(): pl.pallas_call(first_kernel, in_specs=[HB] * 4, out_specs=[VM] * 6, out_s...  3.6 us
    pallas_call x1, Pallas kernels, body(): pl.pallas_call(second_kernel, in_specs=[VM] * 5, out_specs=[HB, VM, VM],...  1.25 us
    pallas_call x1, Pallas kernels, body(): pl.pallas_call(last_kernel, in_specs=[VM] * 4, out_specs=VM, out_shape=ja...  0.9 us
  transfers between devices with their start and end apart: 4, of which 2 were waited for; matrix products, arithmetic and copies ran while one was open for 0% of the time, Pallas kernels for 4%

profile of v3, /device:TPU:1, one launch (start us, length us, event | category | flops | bytes accessed | tf_op | source)
XLA Modules:
  0.0 39.8 jit_solution(14896055655458581848)
XLA Ops:
  0.6 0.0 copy-start
  0.6 3.6 %first.1 = (bf16[512,4096]{1,0:T(8,128)(2,1)S(1)}, f32[32,4096]{1,0:T(8,128)S(1)}, f32[1,4096]{1,0:T(1,128)S(1)}, f32[16,8,128]{2,1,0:T(8,128)S(1)}, f32[32,512]{1,0:T(8,128)S(1)}, /*index=5*/f32[32,128]{1,0:T(8,128)S(1)}) custom-call(bf16[512,4096]{1,0:T(8,128)(2,1)} %s_hbm.1, f32[1,4096]{1,0:T(1,128)} %bitcast.5, f32[16,4096]{1,0:T(8,128)} %hs_hbm.1, ...), custom_call_target="tpu_custom_call" | custom-call | tf_op jit(solution)/shard_map/first/pallas_call | solution.py:159
  4.3 14.9 %all_to_all.10.parts = f32[16,8,128]{2,1,0:T(8,128)S(1)} all-to-all(f32[16,8,128]{2,1,0:T(8,128)S(1)} %get-tuple-element.13), channel_id=1, replica_groups=mesh['rows'=8,'cols'=16] {'cols'}, dimensions={0} | all-to-all | bytes 131072 | tf_op jit(solution)/shard_map/all_to_all | solution.py:175
  19.2 0.0 copy-done
  19.2 1.2 %second.1 = (f32[128,1,128]{2,1,0:T(1,128)}, f32[8,128]{1,0:T(8,128)S(1)}, f32[1,4096]{1,0:T(1,128)S(1)}) custom-call(f32[16,8,128]{2,1,0:T(8,128)S(1)} %all_to_all.10.parts, s32[1,512]{1,0:T(1,128)S(1)} %bitcast.4, f32[32,512]{1,0:T(8,128)S(1)} %get-tuple-element.14.proj, f32[32,128]{1,0:T(8,128)S(1)} %get-tuple-element.15.bias, ...), custom_call_target="tpu_custom_call" | custom-call | tf_op jit(solution)/shard_map/second/pallas_call | solution.py:176
  20.4 7.4 %all-to-all-start.1 = ((f32[128,1,128]{2,1,0:T(1,128)}), f32[128,1,128]{2,1,0:T(1,128)S(1)}, u32[]{:S(2)}, u32[]{:S(2)}) async-start(f32[128,1,128]{2,1,0:T(1,128)} %get-tuple-element.17), calls=%async_computation.1 | async-start | bytes 131072 | tf_op jit(solution)/shard_map/all_to_all | solution.py:189
  27.8 2.9 %collective-permute-start = (f32[1,4096]{1,0:T(1,128)S(1)}, f32[1,4096]{1,0:T(1,128)S(1)}, u32[]{:S(2)}, u32[]{:S(2)}) collective-permute-start(f32[1,4096]{1,0:T(1,128)S(1)} %get-tuple-element.19), channel_id=1, source_target_pairs={{0,112},{16,96},{32,80},{48,64},{64,48},{80,32},{96,16},{112,0},{1... | collective-permute-start | bytes 49160 | tf_op jit(solution)/shard_map/ppermute | solution.py:149
  30.7 1.9 %collective-permute-done = f32[1,4096]{1,0:T(1,128)S(1)} collective-permute-done((f32[1,4096]{1,0:T(1,128)S(1)}, f32[1,4096]{1,0:T(1,128)S(1)}, u32[]{:S(2)}, u32[]{:S(2)}) %collective-permute-start) | collective-permute-done | bytes 16416 | tf_op jit(solution)/shard_map/ppermute | solution.py:149
  32.6 0.3 collective-permute-start.1
  32.9 3.4 %collective-permute-done.1 = f32[1,4096]{1,0:T(1,128)S(1)} collective-permute-done((f32[1,4096]{1,0:T(1,128)S(1)}, f32[1,4096]{1,0:T(1,128)S(1)}, u32[]{:S(2)}, u32[]{:S(2)}) %collective-permute-start.1) | collective-permute-done | bytes 16416 | tf_op jit(solution)/shard_map/ppermute | solution.py:149
  36.3 0.5 %collective-permute-start.2 = (f32[1,4096]{1,0:T(1,128)S(1)}, f32[1,4096]{1,0:T(1,128)S(1)}, u32[]{:S(2)}, u32[]{:S(2)}) collective-permute-start(f32[1,4096]{1,0:T(1,128)S(1)} %add.7.mine), channel_id=1, source_target_pairs={{0,16},{16,0},{32,48},{48,32},{64,80},{80,64},{96,112},{112,96},{1... | collective-permute-start | bytes 49160 | tf_op jit(solution)/shard_map/ppermute | solution.py:149
  37.5 0.8 %solve.1 = f32[40,128]{1,0:T(8,128)S(1)} custom-call(s32[1]{0:T(128)S(6)} %copy.8.counter, f32[8,128]{1,0:T(8,128)S(1)} %get-tuple-element.18.gram), custom_call_target="tpu_custom_call" | custom-call | tf_op jit(solution)/shard_map/solve/pallas_call | solution.py:195
  38.3 0.0 collective-permute-done.2.other
  38.3 0.6 %gradient.1 = (f32[1,4096]{1,0:T(1,128)}, f32[1,4096]{1,0:T(1,128)S(1)}) custom-call(f32[1,4096]{1,0:T(1,128)S(1)} %add.7.mine, f32[1,4096]{1,0:T(1,128)S(1)} %collective-permute-done.2.other, f32[40,128]{1,0:T(8,128)S(1)} %solve.1, f32[1,4096]{1,0:T(1,128)S(1)} %get-tuple-element.20.wrow), custom_call_target="tpu_custom_call" | custom-call | tf_op jit(solution)/shard_map/gradient/pallas_call | solution.py:203
  38.9 0.0 all-to-all-done.1.crosses
  38.9 0.9 %last.1 = f32[1,4096]{1,0:T(1,128)} custom-call(f32[128,1,128]{2,1,0:T(1,128)S(1)} %all-to-all-done.1.crosses, f32[40,128]{1,0:T(8,128)S(1)} %solve.1, f32[1,4096]{1,0:T(1,128)S(1)} %get-tuple-element.21.base, f32[32,4096]{1,0:T(8,128)S(1)} %get-tuple-element.22.hist), custom_call_target="tpu_custom_call" | custom-call | tf_op jit(solution)/shard_map/last/pallas_call | solution.py:211
  (2 shorter events, 0.0 us)
Async XLA Ops:
  0.6 18.5 %copy-start = (s32[512]{0:T(512)S(1)}, s32[512]{0:T(512)}, u32[]{:S(2)}) copy-start(s32[512]{0:T(512)} %param.7) | copy-start | bytes 6148
  20.4 18.5 %all-to-all-start.1 = ((f32[128,1,128]{2,1,0:T(1,128)}), f32[128,1,128]{2,1,0:T(1,128)S(1)}, u32[]{:S(2)}, u32[]{:S(2)}) async-start(f32[128,1,128]{2,1,0:T(1,128)} %get-tuple-element.17), calls=%async_computation.1 | async-start | bytes 131072 | tf_op jit(solution)/shard_map/all_to_all | solution.py:189
  27.8 4.8 %collective-permute-start = (f32[1,4096]{1,0:T(1,128)S(1)}, f32[1,4096]{1,0:T(1,128)S(1)}, u32[]{:S(2)}, u32[]{:S(2)}) collective-permute-start(f32[1,4096]{1,0:T(1,128)S(1)} %get-tuple-element.19), channel_id=1, source_target_pairs={{0,112},{16,96},{32,80},{48,64},{64,48},{80,32},{96,16},{112,0},{1... | collective-permute-start | bytes 49160 | tf_op jit(solution)/shard_map/ppermute | solution.py:149
  32.6 3.7 %collective-permute-start.1 = (f32[1,4096]{1,0:T(1,128)S(1)}, f32[1,4096]{1,0:T(1,128)S(1)}, u32[]{:S(2)}, u32[]{:S(2)}) collective-permute-start(f32[1,4096]{1,0:T(1,128)S(1)} %add.6), channel_id=1, source_target_pairs={{0,48},{16,32},{32,16},{48,0},{64,112},{80,96},{96,80},{112,64},{1... | collective-permute-start | bytes 49160 | tf_op jit(solution)/shard_map/ppermute | solution.py:149
  36.3 2.0 %collective-permute-start.2 = (f32[1,4096]{1,0:T(1,128)S(1)}, f32[1,4096]{1,0:T(1,128)S(1)}, u32[]{:S(2)}, u32[]{:S(2)}) collective-permute-start(f32[1,4096]{1,0:T(1,128)S(1)} %add.7.mine), channel_id=1, source_target_pairs={{0,16},{16,0},{32,48},{48,32},{64,80},{80,64},{96,112},{112,96},{1... | collective-permute-start | bytes 49160 | tf_op jit(solution)/shard_map/ppermute | solution.py:149

commit v4 on v3

--- a/solution.py
+++ b/solution.py
@@ -26,9 +26,8 @@
     return lax.dot_general(left, right, (((1,), (1,)), ((), ())), preferred_element_type=f32)
 
 
-def first_kernel(s_hbm, w_hbm, hs_hbm, hy_hbm, samp, hist, wrow, part, proj, bias, sems):
+def first_kernel(s_hbm, w_hbm, hs_hbm, hy_hbm, samp, hist, wrow, part, sems):
     feats = samp.shape[1]
-    count = samp.shape[0]
     width = feats // CHUNKS
     copies = [
         pltpu.make_async_copy(hs_hbm, hist.at[pl.ds(0, HIST), :], sems.at[0]),
@@ -42,27 +41,22 @@
         copy.start()
     for copy in copies[:3]:
         copy.wait()
-    acc = jnp.zeros((16 + 4 * HIST, count), f32)
-    both = jnp.zeros((4 * HIST, 48), f32)
+    acc = jnp.zeros((16, samp.shape[0]), f32)
+    both = jnp.zeros((4 * HIST, 2 * HIST), f32)
     for c in range(CHUNKS):
         copies[3 + c].wait()
         cols = slice(c * width, (c + 1) * width)
         h = hist[:, cols]
         high = h.astype(bf16)
         low = (h - high.astype(f32)).astype(bf16)
-        w = wrow[:, cols]
-        w16 = w.astype(bf16)
-        w_low = (w - w16.astype(f32)).astype(bf16)
-        w_pair = jnp.where(iota((16, width), 0) == 0, w16.astype(f32), w_low.astype(f32)).astype(bf16)
-        right = jnp.concatenate([high[HIST:], low[HIST:], w_pair], axis=0)
-        left = jnp.concatenate([jnp.broadcast_to(w16, (16, width)), high, low], axis=0)
-        acc = acc + dot_t(left, samp[:, cols])
-        both = both + dot_t(left[16:], right)
-    proj[...] = penalty * (acc[16 : 16 + 2 * HIST] + acc[16 + 2 * HIST :])
-    both = jnp.concatenate([both, jnp.zeros((4 * HIST, 80), f32)], axis=1)
+        left = jnp.concatenate([high, low], axis=0)
+        right = jnp.concatenate([high[HIST:], low[HIST:]], axis=0)
+        both = both + dot_t(left, right)
+        w16 = jnp.broadcast_to(wrow[:, cols].astype(bf16), (16, width))
+        acc = acc + dot_t(w16, samp[:, cols])
+    both = jnp.concatenate([both, jnp.zeros((4 * HIST, 128 - 2 * HIST), f32)], axis=1)
     halves = both[: 2 * HIST] + both[2 * HIST :]
     lane = iota((2 * HIST, 128), 1)
-    bias[...] = jnp.where(jnp.logical_or(lane == 32, lane == 33), 0.125 * halves, 0.0)
     gram = jnp.where(lane < HIST, halves + pltpu.roll(halves, 128 - HIST, 1), 0.0)
     for shift in (16, 32, 64):
         gram = gram + pltpu.roll(gram, shift, 1)
@@ -73,22 +67,27 @@
     part[...] = jnp.broadcast_to(mine[None], part.shape)
 
 
-def second_kernel(parts, labels, proj, bias, samp, cross_hbm, gram, total, cross, sem):
+def second_kernel(parts, labels, samp, hist, wrow, cross_hbm, gram, total, cross, sem):
     summed = jnp.sum(parts[...], axis=0)
     gram[...] = summed
     margin = jnp.concatenate([summed[i : i + 1] for i in range(4)], axis=1)
     resid = (jax.nn.sigmoid(margin) - labels[...].astype(f32)).astype(bf16)
-    prod = proj[...] * resid.astype(f32)
-    acc = bias[...]
-    for i in range(4):
-        acc = acc + prod[:, 128 * i : 128 * i + 128]
-    square = jnp.concatenate([acc, jnp.zeros((96, 128), f32)], axis=0)
+    resid16 = jnp.broadcast_to(resid, (16, resid.shape[1]))
+    width = samp.shape[1] // CHUNKS
+    acc = jnp.zeros((2 * HIST, 128), f32)
+    for c in range(CHUNKS):
+        cols = slice(c * width, (c + 1) * width)
+        t = jnp.dot(resid16, samp[:, cols], preferred_element_type=f32)[0:1]
+        total[:, cols] = t
+        lead = wrow[:, cols] * 0.125 + penalty * t
+        prod = hist[:, cols] * lead
+        for k in range(width // 128):
+            acc = acc + prod[:, 128 * k : 128 * k + 128]
+    square = jnp.concatenate([acc, jnp.zeros((128 - 2 * HIST, 128), f32)], axis=0)
     line = jnp.sum(square.T, axis=0, keepdims=True)
     cross[...] = jnp.broadcast_to(line[None], cross.shape)
     out = pltpu.make_async_copy(cross, cross_hbm, sem)
     out.start()
-    resid16 = jnp.broadcast_to(resid, (16, resid.shape[1]))
-    total[...] = jnp.dot(resid16, samp[...], preferred_element_type=f32)[0:1]
     out.wait()
 
 
@@ -156,17 +155,15 @@
 
 def body(samples, labels, weights, hist_s, hist_y, counter):
     count, feats = samples.shape
-    samp, hist, wrow, part, proj, bias = pl.pallas_call(
+    samp, hist, wrow, part = pl.pallas_call(
         first_kernel,
         in_specs=[HB] * 4,
-        out_specs=[VM] * 6,
+        out_specs=[VM] * 4,
         out_shape=[
             pltpu.VMEM((count, feats), bf16),
             pltpu.VMEM((2 * HIST, feats), f32),
             pltpu.VMEM((1, feats), f32),
             pltpu.VMEM((16, 8, 128), f32),
-            pltpu.VMEM((2 * HIST, count), f32),
-            pltpu.VMEM((2 * HIST, 128), f32),
         ],
         scratch_shapes=[pltpu.SemaphoreType.DMA((3 + CHUNKS,))],
         compiler_params=SMALL,
@@ -185,7 +182,7 @@
         scratch_shapes=[pltpu.VMEM((128, 1, 128), f32), pltpu.SemaphoreType.DMA],
         compiler_params=SMALL,
         name="second",
-    )(parts, labels.reshape(1, count), proj, bias, samp)
+    )(parts, labels.reshape(1, count), samp, hist, wrow)
     crosses = lax.all_to_all(cross, (ROWS, COLS), split_axis=0, concat_axis=0, tiled=True)
     other = swapped(total, 7)
     total = total + other

time: 40 us -> 39.7 us (level)
    pallas_call x1, Pallas kernels: 3.6 us -> 3.12 us  [body(): pl.pallas_call(first_kernel, in_specs=[HB] * 4, out_specs=[VM] * 4, out_s...]
where the time goes in v4:
time: 39.7 us; the launch traced here: 39.5 us
  blocking collectives  14.9 us (38%)
  starting transfers between devices  11.1 us (28%)
  Pallas kernels  6.9 us (17%)
  waiting for transfers between devices  5.3 us (13%)
  between operations  1.33 us (3%)
    all_to_all x1, blocking collectives, body(): parts = lax.all_to_all(part, COLS, split_axis=0, concat_axis=0, tiled=True)  14.9 us
    all_to_all x1, starting transfers between devices, body(): lax.all_to_all(cross, (ROWS, COLS), split_axis=0, concat_axis=0, tiled=True)  7.39 us
    ppermute x3, waiting for transfers between devices, swapped(): return lax.ppermute(array, ROWS, [(i, i ^ mask) for i in range(count)])  5.29 us
    ppermute x3, starting transfers between devices, swapped(): return lax.ppermute(array, ROWS, [(i, i ^ mask) for i in range(count)])  3.69 us
    pallas_call x1, Pallas kernels, body(): pl.pallas_call(first_kernel, in_specs=[HB] * 4, out_specs=[VM] * 4, out_s...  3.12 us
    pallas_call x1, Pallas kernels, body(): pl.pallas_call(second_kernel, in_specs=[VM] * 5, out_specs=[HB, VM, VM],...  1.45 us
    pallas_call x1, Pallas kernels, body(): pl.pallas_call(last_kernel, in_specs=[VM] * 4, out_specs=VM, out_shape=ja...  0.9 us
    pallas_call x1, Pallas kernels, body(): pl.pallas_call(solve_kernel, in_specs=[pl.BlockSpec(memory_space=pltpu.SM...  0.8 us
  transfers between devices with their start and end apart: 4, of which 2 were waited for; matrix products, arithmetic and copies ran while one was open for 0% of the time, Pallas kernels for 4%

profile of v4, /device:TPU:1, one launch (start us, length us, event | category | flops | bytes accessed | tf_op | source)
XLA Modules:
  0.0 39.5 jit_solution(16871293044048018245)
XLA Ops:
  0.6 0.0 copy-start
  0.6 3.1 %first.1 = (bf16[512,4096]{1,0:T(8,128)(2,1)S(1)}, f32[32,4096]{1,0:T(8,128)S(1)}, f32[1,4096]{1,0:T(1,128)S(1)}, f32[16,8,128]{2,1,0:T(8,128)S(1)}) custom-call(bf16[512,4096]{1,0:T(8,128)(2,1)} %s_hbm.1, f32[1,4096]{1,0:T(1,128)} %bitcast.5, f32[16,4096]{1,0:T(8,128)} %hs_hbm.1, f32[16,4096]{1,0:T(8,128)} %hy_hbm.1), custom_call_target="tpu_custom_call" | custom-call | tf_op jit(solution)/shard_map/first/pallas_call | solution.py:158
  3.8 14.9 %all_to_all.10.parts = f32[16,8,128]{2,1,0:T(8,128)S(1)} all-to-all(f32[16,8,128]{2,1,0:T(8,128)S(1)} %get-tuple-element.11), channel_id=1, replica_groups=mesh['rows'=8,'cols'=16] {'cols'}, dimensions={0} | all-to-all | bytes 131072 | tf_op jit(solution)/shard_map/all_to_all | solution.py:172
  18.7 0.0 copy-done
  18.7 1.5 %second.1 = (f32[128,1,128]{2,1,0:T(1,128)}, f32[8,128]{1,0:T(8,128)S(1)}, f32[1,4096]{1,0:T(1,128)S(1)}) custom-call(f32[16,8,128]{2,1,0:T(8,128)S(1)} %all_to_all.10.parts, s32[1,512]{1,0:T(1,128)S(1)} %bitcast.4, bf16[512,4096]{1,0:T(8,128)(2,1)S(1)} %get-tuple-element.12.samp, f32[32,4096]{1,0:T(8,128)S(1)} %get-tuple-element.13.hist, ...), custom_call_target="tpu_custom_call" | custom-call | tf_op jit(solution)/shard_map/second/pallas_call | solution.py:173
  20.1 7.4 %all-to-all-start.1 = ((f32[128,1,128]{2,1,0:T(1,128)}), f32[128,1,128]{2,1,0:T(1,128)S(1)}, u32[]{:S(2)}, u32[]{:S(2)}) async-start(f32[128,1,128]{2,1,0:T(1,128)} %get-tuple-element.15), calls=%async_computation.1 | async-start | bytes 131072 | tf_op jit(solution)/shard_map/all_to_all | solution.py:186
  27.5 2.9 %collective-permute-start = (f32[1,4096]{1,0:T(1,128)S(1)}, f32[1,4096]{1,0:T(1,128)S(1)}, u32[]{:S(2)}, u32[]{:S(2)}) collective-permute-start(f32[1,4096]{1,0:T(1,128)S(1)} %get-tuple-element.17), channel_id=1, source_target_pairs={{0,112},{16,96},{32,80},{48,64},{64,48},{80,32},{96,16},{112,0},{1... | collective-permute-start | bytes 49160 | tf_op jit(solution)/shard_map/ppermute | solution.py:148
  30.5 1.9 %collective-permute-done = f32[1,4096]{1,0:T(1,128)S(1)} collective-permute-done((f32[1,4096]{1,0:T(1,128)S(1)}, f32[1,4096]{1,0:T(1,128)S(1)}, u32[]{:S(2)}, u32[]{:S(2)}) %collective-permute-start) | collective-permute-done | bytes 16416 | tf_op jit(solution)/shard_map/ppermute | solution.py:148
  32.4 0.3 collective-permute-start.1
  32.6 3.4 %collective-permute-done.1 = f32[1,4096]{1,0:T(1,128)S(1)} collective-permute-done((f32[1,4096]{1,0:T(1,128)S(1)}, f32[1,4096]{1,0:T(1,128)S(1)}, u32[]{:S(2)}, u32[]{:S(2)}) %collective-permute-start.1) | collective-permute-done | bytes 16416 | tf_op jit(solution)/shard_map/ppermute | solution.py:148
  36.0 0.5 %collective-permute-start.2 = (f32[1,4096]{1,0:T(1,128)S(1)}, f32[1,4096]{1,0:T(1,128)S(1)}, u32[]{:S(2)}, u32[]{:S(2)}) collective-permute-start(f32[1,4096]{1,0:T(1,128)S(1)} %add.7.mine), channel_id=1, source_target_pairs={{0,16},{16,0},{32,48},{48,32},{64,80},{80,64},{96,112},{112,96},{1... | collective-permute-start | bytes 49160 | tf_op jit(solution)/shard_map/ppermute | solution.py:148
  37.2 0.8 %solve.1 = f32[40,128]{1,0:T(8,128)S(1)} custom-call(s32[1]{0:T(128)S(6)} %copy.8.counter, f32[8,128]{1,0:T(8,128)S(1)} %get-tuple-element.16.gram), custom_call_target="tpu_custom_call" | custom-call | tf_op jit(solution)/shard_map/solve/pallas_call | solution.py:192
  38.0 0.0 collective-permute-done.2.other
  38.0 0.6 %gradient.1 = (f32[1,4096]{1,0:T(1,128)}, f32[1,4096]{1,0:T(1,128)S(1)}) custom-call(f32[1,4096]{1,0:T(1,128)S(1)} %add.7.mine, f32[1,4096]{1,0:T(1,128)S(1)} %collective-permute-done.2.other, f32[40,128]{1,0:T(8,128)S(1)} %solve.1, f32[1,4096]{1,0:T(1,128)S(1)} %get-tuple-element.14.wrow), custom_call_target="tpu_custom_call" | custom-call | tf_op jit(solution)/shard_map/gradient/pallas_call | solution.py:200
  38.6 0.0 all-to-all-done.1.crosses
  38.6 0.9 %last.1 = f32[1,4096]{1,0:T(1,128)} custom-call(f32[128,1,128]{2,1,0:T(1,128)S(1)} %all-to-all-done.1.crosses, f32[40,128]{1,0:T(8,128)S(1)} %solve.1, f32[1,4096]{1,0:T(1,128)S(1)} %get-tuple-element.18.base, f32[32,4096]{1,0:T(8,128)S(1)} %get-tuple-element.13.hist), custom_call_target="tpu_custom_call" | custom-call | tf_op jit(solution)/shard_map/last/pallas_call | solution.py:208
  (2 shorter events, 0.0 us)
Async XLA Ops:
  0.6 18.0 %copy-start = (s32[512]{0:T(512)S(1)}, s32[512]{0:T(512)}, u32[]{:S(2)}) copy-start(s32[512]{0:T(512)} %param.7) | copy-start | bytes 6148
  20.1 18.5 %all-to-all-start.1 = ((f32[128,1,128]{2,1,0:T(1,128)}), f32[128,1,128]{2,1,0:T(1,128)S(1)}, u32[]{:S(2)}, u32[]{:S(2)}) async-start(f32[128,1,128]{2,1,0:T(1,128)} %get-tuple-element.15), calls=%async_computation.1 | async-start | bytes 131072 | tf_op jit(solution)/shard_map/all_to_all | solution.py:186
  27.5 4.8 %collective-permute-start = (f32[1,4096]{1,0:T(1,128)S(1)}, f32[1,4096]{1,0:T(1,128)S(1)}, u32[]{:S(2)}, u32[]{:S(2)}) collective-permute-start(f32[1,4096]{1,0:T(1,128)S(1)} %get-tuple-element.17), channel_id=1, source_target_pairs={{0,112},{16,96},{32,80},{48,64},{64,48},{80,32},{96,16},{112,0},{1... | collective-permute-start | bytes 49160 | tf_op jit(solution)/shard_map/ppermute | solution.py:148
  32.4 3.7 %collective-permute-start.1 = (f32[1,4096]{1,0:T(1,128)S(1)}, f32[1,4096]{1,0:T(1,128)S(1)}, u32[]{:S(2)}, u32[]{:S(2)}) collective-permute-start(f32[1,4096]{1,0:T(1,128)S(1)} %add.6), channel_id=1, source_target_pairs={{0,48},{16,32},{32,16},{48,0},{64,112},{80,96},{96,80},{112,64},{1... | collective-permute-start | bytes 49160 | tf_op jit(solution)/shard_map/ppermute | solution.py:148
  36.0 2.0 %collective-permute-start.2 = (f32[1,4096]{1,0:T(1,128)S(1)}, f32[1,4096]{1,0:T(1,128)S(1)}, u32[]{:S(2)}, u32[]{:S(2)}) collective-permute-start(f32[1,4096]{1,0:T(1,128)S(1)} %add.7.mine), channel_id=1, source_target_pairs={{0,16},{16,0},{32,48},{48,32},{64,80},{80,64},{96,112},{112,96},{1... | collective-permute-start | bytes 49160 | tf_op jit(solution)/shard_map/ppermute | solution.py:148

commit v5 on v4

--- a/solution.py
+++ b/solution.py
@@ -26,34 +26,11 @@
     return lax.dot_general(left, right, (((1,), (1,)), ((), ())), preferred_element_type=f32)
 
 
-def first_kernel(s_hbm, w_hbm, hs_hbm, hy_hbm, samp, hist, wrow, part, sems):
-    feats = samp.shape[1]
-    width = feats // CHUNKS
-    copies = [
-        pltpu.make_async_copy(hs_hbm, hist.at[pl.ds(0, HIST), :], sems.at[0]),
-        pltpu.make_async_copy(hy_hbm, hist.at[pl.ds(HIST, HIST), :], sems.at[1]),
-        pltpu.make_async_copy(w_hbm, wrow, sems.at[2]),
-    ]
-    for c in range(CHUNKS):
-        cols = pl.ds(c * width, width)
-        copies.append(pltpu.make_async_copy(s_hbm.at[:, cols], samp.at[:, cols], sems.at[3 + c]))
-    for copy in copies:
-        copy.start()
-    for copy in copies[:3]:
-        copy.wait()
-    acc = jnp.zeros((16, samp.shape[0]), f32)
-    both = jnp.zeros((4 * HIST, 2 * HIST), f32)
-    for c in range(CHUNKS):
-        copies[3 + c].wait()
-        cols = slice(c * width, (c + 1) * width)
-        h = hist[:, cols]
-        high = h.astype(bf16)
-        low = (h - high.astype(f32)).astype(bf16)
-        left = jnp.concatenate([high, low], axis=0)
-        right = jnp.concatenate([high[HIST:], low[HIST:]], axis=0)
-        both = both + dot_t(left, right)
-        w16 = jnp.broadcast_to(wrow[:, cols].astype(bf16), (16, width))
-        acc = acc + dot_t(w16, samp[:, cols])
+def gram_of(hist):
+    h = hist[...]
+    high = h.astype(bf16)
+    low = (h - high.astype(f32)).astype(bf16)
+    both = dot_t(jnp.concatenate([high, low], axis=0), jnp.concatenate([high[HIST:], low[HIST:]], axis=0))
     both = jnp.concatenate([both, jnp.zeros((4 * HIST, 128 - 2 * HIST), f32)], axis=1)
     halves = both[: 2 * HIST] + both[2 * HIST :]
     lane = iota((2 * HIST, 128), 1)
@@ -61,19 +38,47 @@
     for shift in (16, 32, 64):
         gram = gram + pltpu.roll(gram, shift, 1)
     gram = jnp.where(lane // HIST == iota((2 * HIST, 128), 0) % 8, gram, 0.0)
-    packed = [jnp.sum(gram[8 * a : 8 * a + 8], axis=0, keepdims=True) for a in range(4)]
+    return jnp.concatenate([jnp.sum(gram[8 * a : 8 * a + 8], axis=0, keepdims=True) for a in range(4)], axis=0)
+
+
+def first_kernel(s_hbm, w_hbm, hs_hbm, hy_hbm, samp, hist, wrow, part, sems):
+    feats = samp.shape[1]
+    width = feats // CHUNKS
+    copies = [pltpu.make_async_copy(w_hbm, wrow, sems.at[0])]
+    for c in range(CHUNKS):
+        cols = pl.ds(c * width, width)
+        copies.append(pltpu.make_async_copy(s_hbm.at[:, cols], samp.at[:, cols], sems.at[1 + c]))
+    copies.append(pltpu.make_async_copy(hs_hbm, hist.at[pl.ds(0, HIST), :], sems.at[1 + CHUNKS]))
+    copies.append(pltpu.make_async_copy(hy_hbm, hist.at[pl.ds(HIST, HIST), :], sems.at[2 + CHUNKS]))
+    for copy in copies:
+        copy.start()
+    copies[0].wait()
+    acc = jnp.zeros((16, samp.shape[0]), f32)
+    for c in range(CHUNKS):
+        copies[1 + c].wait()
+        cols = slice(c * width, (c + 1) * width)
+        w16 = jnp.broadcast_to(wrow[:, cols].astype(bf16), (16, width))
+        acc = acc + dot_t(w16, samp[:, cols])
     rows = [acc[0:1, 128 * i : 128 * i + 128] for i in range(4)]
-    mine = jnp.concatenate(rows + packed, axis=0)
+    mine = jnp.concatenate(rows + [jnp.zeros((4, 128), f32)], axis=0)
     part[...] = jnp.broadcast_to(mine[None], part.shape)
-
-
-def second_kernel(parts, labels, samp, hist, wrow, cross_hbm, gram, total, cross, sem):
+    copies[1 + CHUNKS].wait()
+    copies[2 + CHUNKS].wait()
+
+    @pl.when(lax.axis_index(ROWS) % 2 == 1)
+    def _():
+        part[:, 4:8, :] = jnp.broadcast_to(gram_of(hist)[None], (part.shape[0], 4, 128))
+
+
+def second_kernel(parts, labels, samp, hist, wrow, cross_hbm, total, cross, sem):
     summed = jnp.sum(parts[...], axis=0)
-    gram[...] = summed
+    feats = samp.shape[1]
+    for i in range(4):
+        total[:, feats + 128 * i : feats + 128 * i + 128] = summed[4 + i : 5 + i]
     margin = jnp.concatenate([summed[i : i + 1] for i in range(4)], axis=1)
     resid = (jax.nn.sigmoid(margin) - labels[...].astype(f32)).astype(bf16)
     resid16 = jnp.broadcast_to(resid, (16, resid.shape[1]))
-    width = samp.shape[1] // CHUNKS
+    width = feats // CHUNKS
     acc = jnp.zeros((2 * HIST, 128), f32)
     for c in range(CHUNKS):
         cols = slice(c * width, (c + 1) * width)
@@ -98,7 +103,7 @@
     low_lane = lane < HIST
 
     def unpacked(a):
-        kept = jnp.where(iota((8, 128), 1) // HIST == iota((8, 128), 0), gram[4 + a : 5 + a, :], 0.0)
+        kept = jnp.where(iota((8, 128), 1) // HIST == iota((8, 128), 0), gram[:, 128 * a : 128 * a + 128], 0.0)
         for shift in (16, 32, 64):
             kept = kept + pltpu.roll(kept, shift, 1)
         return kept
@@ -170,25 +175,26 @@
         name="first",
     )(*(pltpu.with_memory_space_constraint(a, pltpu.HBM) for a in (samples, weights.reshape(1, feats), hist_s, hist_y)))
     parts = lax.all_to_all(part, COLS, split_axis=0, concat_axis=0, tiled=True)
-    cross, gram, total = pl.pallas_call(
+    cross, total = pl.pallas_call(
         second_kernel,
         in_specs=[VM] * 5,
-        out_specs=[HB, VM, VM],
+        out_specs=[HB, VM],
         out_shape=[
             jax.ShapeDtypeStruct((128, 1, 128), f32),
-            pltpu.VMEM((8, 128), f32),
-            pltpu.VMEM((1, feats), f32),
+            pltpu.VMEM((1, feats + 512), f32),
         ],
         scratch_shapes=[pltpu.VMEM((128, 1, 128), f32), pltpu.SemaphoreType.DMA],
         compiler_params=SMALL,
         name="second",
     )(parts, labels.reshape(1, count), samp, hist, wrow)
     crosses = lax.all_to_all(cross, (ROWS, COLS), split_axis=0, concat_axis=0, tiled=True)
-    other = swapped(total, 7)
+    other = swapped(total, 1)
     total = total + other
+    gram = total[:, feats:]
+    total = total[:, :feats]
     other = swapped(total, 3)
     total = total + other
-    other = swapped(total, 1)
+    other = swapped(total, 7)
     solve = pl.pallas_call(
         solve_kernel,
         in_specs=[pl.BlockSpec(memory_space=pltpu.SMEM), VM],
@@ -201,7 +207,7 @@
         gradient_kernel,
         in_specs=[VM] * 4,
         out_specs=[VM] * 2,
-        out_shape=[jax.ShapeDtypeStruct((1, feats), f32), pltpu.VMEM((1, feats), f32)],
+        out_shape=[pltpu.VMEM((1, feats), f32), pltpu.VMEM((1, feats), f32)],
         compiler_params=SMALL,
         name="gradient",
     )(total, other, solve, wrow)

time: 39.7 us -> 40.2 us (1.013)
  local copies, waits for them, and re-layouts: 0.01 us -> 0.62 us
  Pallas kernels: 6.9 us -> 6.38 us
    all_to_all x1, waiting for transfers between devices: 0.01 us -> 4.28 us  [body(): lax.all_to_all(cross, (ROWS, COLS), split_axis=0, concat_axis=0, tiled=True)]
    ppermute x3, waiting for transfers between devices: 5.29 us -> 1.26 us  [swapped(): return lax.ppermute(array, ROWS, [(i, i ^ mask) for i in range(count)])]
    ppermute x3, starting transfers between devices: 3.69 us -> 6.06 us  [swapped(): return lax.ppermute(array, ROWS, [(i, i ^ mask) for i in range(count)])]
    all_to_all x1, starting transfers between devices: 7.39 us -> 5.15 us  [body(): lax.all_to_all(cross, (ROWS, COLS), split_axis=0, concat_axis=0, tiled=True)]
    unnamed x2 -> x3, local copies, waits for them, and re-layouts: 0.01 us -> 0.61 us
    pallas_call x1, Pallas kernels: 0.63 us -> 0.09 us  [body(): pl.pallas_call(gradient_kernel, in_specs=[VM] * 4, out_specs=[VM] * 2, ou...]
  transfers between devices with their start and end apart: 4 -> 4, of which waited for: 2 -> 3; matrix products, arithmetic and copies ran while one was open for 0% -> 2% of each run, Pallas kernels for 4% -> 2%
where the time goes in v5:
time: 40.2 us; the launch traced here: 40 us
  blocking collectives  14.9 us (37%)
  starting transfers between devices  11.2 us (28%)
  Pallas kernels  6.38 us (16%)
  waiting for transfers between devices  5.53 us (14%)
  between operations  1.36 us (3%)
  local copies, waits for them, and re-layouts  0.62 us (2%)
    all_to_all x1, blocking collectives, body(): parts = lax.all_to_all(part, COLS, split_axis=0, concat_axis=0, tiled=True)  14.9 us
    ppermute x3, starting transfers between devices, swapped(): return lax.ppermute(array, ROWS, [(i, i ^ mask) for i in range(count)])  6.06 us
    all_to_all x1, starting transfers between devices, body(): lax.all_to_all(cross, (ROWS, COLS), split_axis=0, concat_axis=0, tiled=True)  5.15 us
    all_to_all x1, waiting for transfers between devices, body(): lax.all_to_all(cross, (ROWS, COLS), split_axis=0, concat_axis=0, tiled=True)  4.28 us
    pallas_call x1, Pallas kernels, body(): pl.pallas_call(first_kernel, in_specs=[HB] * 4, out_specs=[VM] * 4, out_s...  3.14 us
    pallas_call x1, Pallas kernels, body(): pl.pallas_call(second_kernel, in_specs=[VM] * 5, out_specs=[HB, VM], out_...  1.45 us
    ppermute x3, waiting for transfers between devices, swapped(): return lax.ppermute(array, ROWS, [(i, i ^ mask) for i in range(count)])  1.26 us
    pallas_call x1, Pallas kernels, body(): pl.pallas_call(last_kernel, in_specs=[VM] * 4, out_specs=VM, out_shape=ja...  0.9 us
  transfers between devices with their start and end apart: 4, of which 3 were waited for; matrix products, arithmetic and copies ran while one was open for 2% of the time, Pallas kernels for 2%

profile of v5, /device:TPU:1, one launch (start us, length us, event | category | flops | bytes accessed | tf_op | source)
XLA Modules:
  0.0 40.0 jit_solution(6843875407756487405)
XLA Ops:
  0.6 0.0 copy-start
  0.6 3.1 %first.1 = (bf16[512,4096]{1,0:T(8,128)(2,1)S(1)}, f32[32,4096]{1,0:T(8,128)S(1)}, f32[1,4096]{1,0:T(1,128)S(1)}, f32[16,8,128]{2,1,0:T(8,128)S(1)}) custom-call(bf16[512,4096]{1,0:T(8,128)(2,1)} %s_hbm.1, f32[1,4096]{1,0:T(1,128)} %bitcast.6, f32[16,4096]{1,0:T(8,128)} %hs_hbm.1, f32[16,4096]{1,0:T(8,128)} %hy_hbm.1), custom_call_target="tpu_custom_call" | custom-call | tf_op jit(solution)/shard_map/first/pallas_call | solution.py:163
  3.8 14.9 %all_to_all.10.parts = f32[16,8,128]{2,1,0:T(8,128)S(1)} all-to-all(f32[16,8,128]{2,1,0:T(8,128)S(1)} %get-tuple-element.10), channel_id=1, replica_groups=mesh['rows'=8,'cols'=16] {'cols'}, dimensions={0} | all-to-all | bytes 131072 | tf_op jit(solution)/shard_map/all_to_all | solution.py:177
  18.7 0.0 copy-done
  18.7 1.5 %second.1 = (f32[128,1,128]{2,1,0:T(1,128)}, f32[1,4608]{1,0:T(1,128)S(1)}) custom-call(f32[16,8,128]{2,1,0:T(8,128)S(1)} %all_to_all.10.parts, s32[1,512]{1,0:T(1,128)S(1)} %bitcast.5, bf16[512,4096]{1,0:T(8,128)(2,1)S(1)} %get-tuple-element.11.samp, f32[32,4096]{1,0:T(8,128)S(1)} %get-tuple-element.12.hist, f32[1,4096]{1,0:T(1,128)S(1)} %get-tuple-element.13.wrow), custom_call_target="tpu_custom_call" | custom-call | tf_op jit(solution)/shard_map/second/pallas_call | solution.py:178
  20.2 1.6 %collective-permute-start = (f32[1,4608]{1,0:T(1,128)S(1)}, f32[1,4608]{1,0:T(1,128)S(1)}, u32[]{:S(2)}, u32[]{:S(2)}) collective-permute-start(f32[1,4608]{1,0:T(1,128)S(1)} %get-tuple-element.15), channel_id=1, source_target_pairs={{0,16},{16,0},{32,48},{48,32},{64,80},{80,64},{96,112},{112,96},{1... | collective-permute-start | bytes 55304 | tf_op jit(solution)/shard_map/ppermute | solution.py:153
  21.8 0.8 %collective-permute-done = f32[1,4608]{1,0:T(1,128)S(1)} collective-permute-done((f32[1,4608]{1,0:T(1,128)S(1)}, f32[1,4608]{1,0:T(1,128)S(1)}, u32[]{:S(2)}, u32[]{:S(2)}) %collective-permute-start) | collective-permute-done | bytes 18464 | tf_op jit(solution)/shard_map/ppermute | solution.py:153
  22.6 1.5 %collective-permute-start.1 = (f32[1,4096]{1,0:T(1,128)S(1)}, f32[1,4096]{1,0:T(1,128)S(1)}, u32[]{:S(2)}, u32[]{:S(2)}) collective-permute-start(f32[1,4096]{1,0:T(1,128)S(1)} %slice.9), channel_id=1, source_target_pairs={{0,48},{16,32},{32,16},{48,0},{64,112},{80,96},{96,80},{112,64},{1... | collective-permute-start | bytes 49160 | tf_op jit(solution)/shard_map/ppermute | solution.py:153
  24.2 5.1 %all-to-all-start.1 = ((f32[128,1,128]{2,1,0:T(1,128)}), f32[128,1,128]{2,1,0:T(1,128)S(1)}, u32[]{:S(2)}, u32[]{:S(2)}) async-start(f32[128,1,128]{2,1,0:T(1,128)} %get-tuple-element.14), calls=%async_computation.1 | async-start | bytes 131072 | tf_op jit(solution)/shard_map/all_to_all | solution.py:190
  29.3 0.0 collective-permute-done.1
  29.4 2.9 %collective-permute-start.2 = (f32[1,4096]{1,0:T(1,128)S(1)}, f32[1,4096]{1,0:T(1,128)S(1)}, u32[]{:S(2)}, u32[]{:S(2)}) collective-permute-start(f32[1,4096]{1,0:T(1,128)S(1)} %slice_add_fusion.mine), channel_id=1, source_target_pairs={{0,112},{16,96},{32,80},{48,64},{64,48},{80,32},{96,16},{112,0},{1... | collective-permute-start | bytes 49160 | tf_op jit(solution)/shard_map/ppermute | solution.py:153
  33.0 0.8 %solve.1 = f32[40,128]{1,0:T(8,128)S(1)} custom-call(s32[1]{0:T(128)S(6)} %copy.9.counter, f32[1,512]{1,0:T(1,128)S(1)} %slice.8.gram), custom_call_target="tpu_custom_call" | custom-call | tf_op jit(solution)/shard_map/solve/pallas_call | solution.py:198
  33.8 0.4 %collective-permute-done.2.other = f32[1,4096]{1,0:T(1,128)S(1)} collective-permute-done((f32[1,4096]{1,0:T(1,128)S(1)}, f32[1,4096]{1,0:T(1,128)S(1)}, u32[]{:S(2)}, u32[]{:S(2)}) %collective-permute-start.2) | collective-permute-done | bytes 16416 | tf_op jit(solution)/shard_map/ppermute | solution.py:153
  34.2 0.1 gradient.1
  34.3 0.6 %copy.8 = f32[4096]{0:T(1024)} copy(f32[4096]{0:T(1024)S(1)} %bitcast.4) | data formatting | bytes 32768
  34.9 4.3 %all-to-all-done.1.crosses = f32[128,1,128]{2,1,0:T(1,128)S(1)} async-done(((f32[128,1,128]{2,1,0:T(1,128)}), f32[128,1,128]{2,1,0:T(1,128)S(1)}, u32[]{:S(2)}, u32[]{:S(2)}) %all-to-all-start.1) | async-done | bytes 65568 | tf_op jit(solution)/shard_map/all_to_all | solution.py:190
  39.1 0.9 %last.1 = f32[1,4096]{1,0:T(1,128)} custom-call(f32[128,1,128]{2,1,0:T(1,128)S(1)} %all-to-all-done.1.crosses, f32[40,128]{1,0:T(8,128)S(1)} %solve.1, f32[1,4096]{1,0:T(1,128)S(1)} %get-tuple-element.16.base, f32[32,4096]{1,0:T(8,128)S(1)} %get-tuple-element.12.hist), custom_call_target="tpu_custom_call" | custom-call | tf_op jit(solution)/shard_map/last/pallas_call | solution.py:214
  (4 shorter events, 0.0 us)
Async XLA Ops:
  0.6 18.1 %copy-start = (s32[512]{0:T(512)S(1)}, s32[512]{0:T(512)}, u32[]{:S(2)}) copy-start(s32[512]{0:T(512)} %param.7) | copy-start | bytes 6148
  20.2 2.5 %collective-permute-start = (f32[1,4608]{1,0:T(1,128)S(1)}, f32[1,4608]{1,0:T(1,128)S(1)}, u32[]{:S(2)}, u32[]{:S(2)}) collective-permute-start(f32[1,4608]{1,0:T(1,128)S(1)} %get-tuple-element.15), channel_id=1, source_target_pairs={{0,16},{16,0},{32,48},{48,32},{64,80},{80,64},{96,112},{112,96},{1... | collective-permute-start | bytes 55304 | tf_op jit(solution)/shard_map/ppermute | solution.py:153
  22.6 6.7 %collective-permute-start.1 = (f32[1,4096]{1,0:T(1,128)S(1)}, f32[1,4096]{1,0:T(1,128)S(1)}, u32[]{:S(2)}, u32[]{:S(2)}) collective-permute-start(f32[1,4096]{1,0:T(1,128)S(1)} %slice.9), channel_id=1, source_target_pairs={{0,48},{16,32},{32,16},{48,0},{64,112},{80,96},{96,80},{112,64},{1... | collective-permute-start | bytes 49160 | tf_op jit(solution)/shard_map/ppermute | solution.py:153
  24.2 15.0 %all-to-all-start.1 = ((f32[128,1,128]{2,1,0:T(1,128)}), f32[128,1,128]{2,1,0:T(1,128)S(1)}, u32[]{:S(2)}, u32[]{:S(2)}) async-start(f32[128,1,128]{2,1,0:T(1,128)} %get-tuple-element.14), calls=%async_computation.1 | async-start | bytes 131072 | tf_op jit(solution)/shard_map/all_to_all | solution.py:190
  29.4 4.8 %collective-permute-start.2 = (f32[1,4096]{1,0:T(1,128)S(1)}, f32[1,4096]{1,0:T(1,128)S(1)}, u32[]{:S(2)}, u32[]{:S(2)}) collective-permute-start(f32[1,4096]{1,0:T(1,128)S(1)} %slice_add_fusion.mine), channel_id=1, source_target_pairs={{0,112},{16,96},{32,80},{48,64},{64,48},{80,32},{96,16},{112,0},{1... | collective-permute-start | bytes 49160 | tf_op jit(solution)/shard_map/ppermute | solution.py:153

commit v6 on v5

--- a/solution.py
+++ b/solution.py
@@ -143,7 +143,7 @@
 
 
 def last_kernel(crosses, solve, base, hist, new_weights):
-    line = jnp.sum(crosses[...], axis=0)
+    line = jnp.sum(jnp.sum(crosses[...], axis=0), axis=0, keepdims=True)
     coefs = step_length * jnp.sum(solve[0 : 2 * HIST, :] * line, axis=1, keepdims=True)
     new_weights[...] = base[...] - jnp.sum(hist[...] * coefs, axis=0, keepdims=True)
 
@@ -174,7 +174,7 @@
         compiler_params=SMALL,
         name="first",
     )(*(pltpu.with_memory_space_constraint(a, pltpu.HBM) for a in (samples, weights.reshape(1, feats), hist_s, hist_y)))
-    parts = lax.all_to_all(part, COLS, split_axis=0, concat_axis=0, tiled=True)
+    parts = lax.all_to_all(part, COLS, split_axis=0, concat_axis=0, axis_index_groups=[[15] + [i for i in range(16) if i != 15]], tiled=True)
     cross, total = pl.pallas_call(
         second_kernel,
         in_specs=[VM] * 5,
@@ -187,7 +187,7 @@
         compiler_params=SMALL,
         name="second",
     )(parts, labels.reshape(1, count), samp, hist, wrow)
-    crosses = lax.all_to_all(cross, (ROWS, COLS), split_axis=0, concat_axis=0, tiled=True)
+    crosses = lax.all_to_all(cross, (ROWS, COLS), split_axis=0, concat_axis=0, axis_index_groups=[list(range(127, -1, -1))], tiled=True)
     other = swapped(total, 1)
     total = total + other
     gram = total[:, feats:]
@@ -218,7 +218,7 @@
         out_shape=jax.ShapeDtypeStruct((1, feats), f32),
         compiler_params=SMALL,
         name="last",
-    )(crosses, solve, base, hist)
+    )(crosses.reshape(16, 8, 128), solve, base, hist)
     return new_weights.reshape(feats), gradient.reshape(feats)
 
 

time: 40.2 us -> 39 us (0.970)
  blocking collectives: 14.9 us -> 12.8 us
  starting transfers between devices: 11.2 us -> 12.5 us
    all_to_all x1, blocking collectives: 14.9 us -> 12.8 us  [body(): lax.all_to_all(part, COLS, split_axis=0, concat_axis=0, axis_index_groups...]
    all_to_all x1, starting transfers between devices: 5.15 us -> 6.77 us  [body(): lax.all_to_all(cross, (ROWS, COLS), split_axis=0, concat_axis=0, axis_ind...]
where the time goes in v6:
time: 39 us; the launch traced here: 38.8 us
  blocking collectives  12.8 us (33%)
  starting transfers between devices  12.5 us (32%)
  Pallas kernels  6.26 us (16%)
  waiting for transfers between devices  5.21 us (13%)
  between operations  1.36 us (3%)
  local copies, waits for them, and re-layouts  0.62 us (2%)
    all_to_all x1, blocking collectives, body(): lax.all_to_all(part, COLS, split_axis=0, concat_axis=0, axis_index_groups...  12.8 us
    all_to_all x1, starting transfers between devices, body(): lax.all_to_all(cross, (ROWS, COLS), split_axis=0, concat_axis=0, axis_ind...  6.77 us
    ppermute x3, starting transfers between devices, swapped(): return lax.ppermute(array, ROWS, [(i, i ^ mask) for i in range(count)])  5.75 us
    all_to_all x1, waiting for transfers between devices, body(): lax.all_to_all(cross, (ROWS, COLS), split_axis=0, concat_axis=0, axis_ind...  3.98 us
    pallas_call x1, Pallas kernels, body(): pl.pallas_call(first_kernel, in_specs=[HB] * 4, out_specs=[VM] * 4, out_s...  3.14 us
    pallas_call x1, Pallas kernels, body(): pl.pallas_call(second_kernel, in_specs=[VM] * 5, out_specs=[HB, VM], out_...  1.45 us
    ppermute x3, waiting for transfers between devices, swapped(): return lax.ppermute(array, ROWS, [(i, i ^ mask) for i in range(count)])  1.23 us
    pallas_call x1, Pallas kernels, body(): pl.pallas_call(solve_kernel, in_specs=[pl.BlockSpec(memory_space=pltpu.SM...  0.8 us
  transfers between devices with their start and end apart: 4, of which 3 were waited for; matrix products, arithmetic and copies ran while one was open for 2% of the time, Pallas kernels for 2%

profile of v6, /device:TPU:1, one launch (start us, length us, event | category | flops | bytes accessed | tf_op | source)
XLA Modules:
  0.0 38.8 jit_solution(110760415459990261)
XLA Ops:
  0.6 0.0 copy-start
  0.6 3.1 %first.1 = (bf16[512,4096]{1,0:T(8,128)(2,1)S(1)}, f32[32,4096]{1,0:T(8,128)S(1)}, f32[1,4096]{1,0:T(1,128)S(1)}, f32[16,8,128]{2,1,0:T(8,128)S(1)}) custom-call(bf16[512,4096]{1,0:T(8,128)(2,1)} %s_hbm.1, f32[1,4096]{1,0:T(1,128)} %bitcast.8, f32[16,4096]{1,0:T(8,128)} %hs_hbm.1, f32[16,4096]{1,0:T(8,128)} %hy_hbm.1), custom_call_target="tpu_custom_call" | custom-call | tf_op jit(solution)/shard_map/first/pallas_call | solution.py:163
  3.8 12.8 %all_to_all.10.parts = f32[16,8,128]{2,1,0:T(8,128)S(1)} all-to-all(f32[16,8,128]{2,1,0:T(8,128)S(1)} %get-tuple-element.10), channel_id=1, replica_groups={{15,0,1,2,3,4,5,6,7,8,9,10,11,12,13,14},{31,16,17,18,19,20,21,22,23,24,..., dimensions={0} | all-to-all | bytes 131072 | tf_op jit(solution)/shard_map/all_to_all | solution.py:177
  16.6 0.0 copy-done
  16.6 1.5 %second.1 = (f32[128,1,128]{2,1,0:T(1,128)}, f32[1,4608]{1,0:T(1,128)S(1)}) custom-call(f32[16,8,128]{2,1,0:T(8,128)S(1)} %all_to_all.10.parts, s32[1,512]{1,0:T(1,128)S(1)} %bitcast.7, bf16[512,4096]{1,0:T(8,128)(2,1)S(1)} %get-tuple-element.11.samp, f32[32,4096]{1,0:T(8,128)S(1)} %get-tuple-element.12.hist, f32[1,4096]{1,0:T(1,128)S(1)} %get-tuple-element.13.wrow), custom_call_target="tpu_custom_call" | custom-call | tf_op jit(solution)/shard_map/second/pallas_call | solution.py:178
  18.1 1.3 %collective-permute-start = (f32[1,4608]{1,0:T(1,128)S(1)}, f32[1,4608]{1,0:T(1,128)S(1)}, u32[]{:S(2)}, u32[]{:S(2)}) collective-permute-start(f32[1,4608]{1,0:T(1,128)S(1)} %get-tuple-element.15), channel_id=1, source_target_pairs={{0,16},{16,0},{32,48},{48,32},{64,80},{80,64},{96,112},{112,96},{1... | collective-permute-start | bytes 55304 | tf_op jit(solution)/shard_map/ppermute | solution.py:153
  19.4 0.8 %collective-permute-done = f32[1,4608]{1,0:T(1,128)S(1)} collective-permute-done((f32[1,4608]{1,0:T(1,128)S(1)}, f32[1,4608]{1,0:T(1,128)S(1)}, u32[]{:S(2)}, u32[]{:S(2)}) %collective-permute-start) | collective-permute-done | bytes 18464 | tf_op jit(solution)/shard_map/ppermute | solution.py:153
  20.2 1.5 %collective-permute-start.1 = (f32[1,4096]{1,0:T(1,128)S(1)}, f32[1,4096]{1,0:T(1,128)S(1)}, u32[]{:S(2)}, u32[]{:S(2)}) collective-permute-start(f32[1,4096]{1,0:T(1,128)S(1)} %slice.9), channel_id=1, source_target_pairs={{0,48},{16,32},{32,16},{48,0},{64,112},{80,96},{96,80},{112,64},{1... | collective-permute-start | bytes 49160 | tf_op jit(solution)/shard_map/ppermute | solution.py:153
  21.8 6.8 %all-to-all-start.1 = ((f32[128,1,128]{2,1,0:T(1,128)}), f32[128,1,128]{2,1,0:T(1,128)S(1)}, u32[]{:S(2)}, u32[]{:S(2)}) async-start(f32[128,1,128]{2,1,0:T(1,128)} %get-tuple-element.14), calls=%async_computation.1 | async-start | bytes 131072 | tf_op jit(solution)/shard_map/all_to_all | solution.py:190
  28.5 0.0 collective-permute-done.1
  28.6 2.9 %collective-permute-start.2 = (f32[1,4096]{1,0:T(1,128)S(1)}, f32[1,4096]{1,0:T(1,128)S(1)}, u32[]{:S(2)}, u32[]{:S(2)}) collective-permute-start(f32[1,4096]{1,0:T(1,128)S(1)} %slice_add_fusion.mine), channel_id=1, source_target_pairs={{0,112},{16,96},{32,80},{48,64},{64,48},{80,32},{96,16},{112,0},{1... | collective-permute-start | bytes 49160 | tf_op jit(solution)/shard_map/ppermute | solution.py:153
  32.2 0.8 %solve.1 = f32[40,128]{1,0:T(8,128)S(1)} custom-call(s32[1]{0:T(128)S(6)} %copy.9.counter, f32[1,512]{1,0:T(1,128)S(1)} %slice.8.gram), custom_call_target="tpu_custom_call" | custom-call | tf_op jit(solution)/shard_map/solve/pallas_call | solution.py:198
  33.0 0.4 %collective-permute-done.2.other = f32[1,4096]{1,0:T(1,128)S(1)} collective-permute-done((f32[1,4096]{1,0:T(1,128)S(1)}, f32[1,4096]{1,0:T(1,128)S(1)}, u32[]{:S(2)}, u32[]{:S(2)}) %collective-permute-start.2) | collective-permute-done | bytes 16416 | tf_op jit(solution)/shard_map/ppermute | solution.py:153
  33.4 0.1 gradient.1
  33.4 0.6 %copy.8 = f32[4096]{0:T(1024)} copy(f32[4096]{0:T(1024)S(1)} %bitcast.5) | data formatting | bytes 32768
  34.1 4.0 %all-to-all-done.1 = f32[128,1,128]{2,1,0:T(1,128)S(1)} async-done(((f32[128,1,128]{2,1,0:T(1,128)}), f32[128,1,128]{2,1,0:T(1,128)S(1)}, u32[]{:S(2)}, u32[]{:S(2)}) %all-to-all-start.1) | async-done | bytes 65568 | tf_op jit(solution)/shard_map/all_to_all | solution.py:190
  38.0 0.8 %last.1 = f32[1,4096]{1,0:T(1,128)} custom-call(f32[16,8,128]{2,1,0:T(8,128)S(1)} %bitcast.6, f32[40,128]{1,0:T(8,128)S(1)} %solve.1, f32[1,4096]{1,0:T(1,128)S(1)} %get-tuple-element.16.base, f32[32,4096]{1,0:T(8,128)S(1)} %get-tuple-element.12.hist), custom_call_target="tpu_custom_call" | custom-call | tf_op jit(solution)/shard_map/last/pallas_call | solution.py:214
  (4 shorter events, 0.0 us)
Async XLA Ops:
  0.6 16.0 %copy-start = (s32[512]{0:T(512)S(1)}, s32[512]{0:T(512)}, u32[]{:S(2)}) copy-start(s32[512]{0:T(512)} %param.7) | copy-start | bytes 6148
  18.1 2.1 %collective-permute-start = (f32[1,4608]{1,0:T(1,128)S(1)}, f32[1,4608]{1,0:T(1,128)S(1)}, u32[]{:S(2)}, u32[]{:S(2)}) collective-permute-start(f32[1,4608]{1,0:T(1,128)S(1)} %get-tuple-element.15), channel_id=1, source_target_pairs={{0,16},{16,0},{32,48},{48,32},{64,80},{80,64},{96,112},{112,96},{1... | collective-permute-start | bytes 55304 | tf_op jit(solution)/shard_map/ppermute | solution.py:153
  20.2 8.3 %collective-permute-start.1 = (f32[1,4096]{1,0:T(1,128)S(1)}, f32[1,4096]{1,0:T(1,128)S(1)}, u32[]{:S(2)}, u32[]{:S(2)}) collective-permute-start(f32[1,4096]{1,0:T(1,128)S(1)} %slice.9), channel_id=1, source_target_pairs={{0,48},{16,32},{32,16},{48,0},{64,112},{80,96},{96,80},{112,64},{1... | collective-permute-start | bytes 49160 | tf_op jit(solution)/shard_map/ppermute | solution.py:153
  21.8 16.3 %all-to-all-start.1 = ((f32[128,1,128]{2,1,0:T(1,128)}), f32[128,1,128]{2,1,0:T(1,128)S(1)}, u32[]{:S(2)}, u32[]{:S(2)}) async-start(f32[128,1,128]{2,1,0:T(1,128)} %get-tuple-element.14), calls=%async_computation.1 | async-start | bytes 131072 | tf_op jit(solution)/shard_map/all_to_all | solution.py:190
  28.6 4.8 %collective-permute-start.2 = (f32[1,4096]{1,0:T(1,128)S(1)}, f32[1,4096]{1,0:T(1,128)S(1)}, u32[]{:S(2)}, u32[]{:S(2)}) collective-permute-start(f32[1,4096]{1,0:T(1,128)S(1)} %slice_add_fusion.mine), channel_id=1, source_target_pairs={{0,112},{16,96},{32,80},{48,64},{64,48},{80,32},{96,16},{112,0},{1... | collective-permute-start | bytes 49160 | tf_op jit(solution)/shard_map/ppermute | solution.py:153

commit v7 on v6

--- a/solution.py
+++ b/solution.py
@@ -3,11 +3,12 @@
 from jax import lax
 from jax.experimental import pallas as pl
 from jax.experimental.pallas import tpu as pltpu
+from jax.sharding import Mesh
 from jax.sharding import PartitionSpec as P
 
 
 HIST = 16
-ROWS = "rows"
+ROWS = ("x", "core")
 COLS = "cols"
 CHUNKS = 8
 
@@ -65,16 +66,16 @@
     copies[1 + CHUNKS].wait()
     copies[2 + CHUNKS].wait()
 
-    @pl.when(lax.axis_index(ROWS) % 2 == 1)
+    @pl.when(lax.axis_index("core") == 1)
     def _():
         part[:, 4:8, :] = jnp.broadcast_to(gram_of(hist)[None], (part.shape[0], 4, 128))
 
 
-def second_kernel(parts, labels, samp, hist, wrow, cross_hbm, total, cross, sem):
+def second_kernel(parts, labels, samp, hist, wrow, packed):
     summed = jnp.sum(parts[...], axis=0)
     feats = samp.shape[1]
     for i in range(4):
-        total[:, feats + 128 * i : feats + 128 * i + 128] = summed[4 + i : 5 + i]
+        packed[:, feats + 128 * i : feats + 128 * i + 128] = summed[4 + i : 5 + i]
     margin = jnp.concatenate([summed[i : i + 1] for i in range(4)], axis=1)
     resid = (jax.nn.sigmoid(margin) - labels[...].astype(f32)).astype(bf16)
     resid16 = jnp.broadcast_to(resid, (16, resid.shape[1]))
@@ -83,16 +84,23 @@
     for c in range(CHUNKS):
         cols = slice(c * width, (c + 1) * width)
         t = jnp.dot(resid16, samp[:, cols], preferred_element_type=f32)[0:1]
-        total[:, cols] = t
+        packed[:, cols] = t
         lead = wrow[:, cols] * 0.125 + penalty * t
         prod = hist[:, cols] * lead
         for k in range(width // 128):
             acc = acc + prod[:, 128 * k : 128 * k + 128]
     square = jnp.concatenate([acc, jnp.zeros((128 - 2 * HIST, 128), f32)], axis=0)
-    line = jnp.sum(square.T, axis=0, keepdims=True)
+    packed[:, feats + 512 :] = jnp.sum(square.T, axis=0, keepdims=True)
+
+
+def spread_kernel(mine, other, cross_hbm, total, gram, cross, sem):
+    feats = total.shape[1]
+    line = mine[:, feats + 512 :] + other[:, feats + 512 :]
     cross[...] = jnp.broadcast_to(line[None], cross.shape)
     out = pltpu.make_async_copy(cross, cross_hbm, sem)
     out.start()
+    total[...] = mine[:, :feats] + other[:, :feats]
+    gram[...] = mine[:, feats : feats + 512] + other[:, feats : feats + 512]
     out.wait()
 
 
@@ -135,17 +143,14 @@
     out[2 * HIST :, :] = jnp.broadcast_to(gamma, (8, 128))
 
 
-def gradient_kernel(mine, other, solve, wrow, gradient, base):
+def last_kernel(crosses, solve, mine, other, wrow, hist, new_weights, gradient):
+    line = jnp.sum(jnp.sum(crosses[...], axis=0), axis=0, keepdims=True)
+    coefs = step_length * jnp.sum(solve[0 : 2 * HIST, :] * line, axis=1, keepdims=True)
     weights = wrow[...]
     grad = weights + penalty * (mine[...] + other[...])
     gradient[...] = grad
-    base[...] = weights - (step_length * solve[2 * HIST : 2 * HIST + 1, 0:1]) * grad
-
-
-def last_kernel(crosses, solve, base, hist, new_weights):
-    line = jnp.sum(jnp.sum(crosses[...], axis=0), axis=0, keepdims=True)
-    coefs = step_length * jnp.sum(solve[0 : 2 * HIST, :] * line, axis=1, keepdims=True)
-    new_weights[...] = base[...] - jnp.sum(hist[...] * coefs, axis=0, keepdims=True)
+    base = weights - (step_length * solve[2 * HIST : 2 * HIST + 1, 0:1]) * grad
+    new_weights[...] = base - jnp.sum(hist[...] * coefs, axis=0, keepdims=True)
 
 
 def swapped(array, mask):
@@ -174,27 +179,33 @@
         compiler_params=SMALL,
         name="first",
     )(*(pltpu.with_memory_space_constraint(a, pltpu.HBM) for a in (samples, weights.reshape(1, feats), hist_s, hist_y)))
-    parts = lax.all_to_all(part, COLS, split_axis=0, concat_axis=0, axis_index_groups=[[15] + [i for i in range(16) if i != 15]], tiled=True)
-    cross, total = pl.pallas_call(
+    parts = lax.all_to_all(part, COLS, split_axis=0, concat_axis=0, axis_index_groups=[[15] + list(range(15))], tiled=True)
+    packed = pl.pallas_call(
         second_kernel,
         in_specs=[VM] * 5,
-        out_specs=[HB, VM],
-        out_shape=[
-            jax.ShapeDtypeStruct((128, 1, 128), f32),
-            pltpu.VMEM((1, feats + 512), f32),
-        ],
-        scratch_shapes=[pltpu.VMEM((128, 1, 128), f32), pltpu.SemaphoreType.DMA],
+        out_specs=VM,
+        out_shape=pltpu.VMEM((1, feats + 640), f32),
         compiler_params=SMALL,
         name="second",
     )(parts, labels.reshape(1, count), samp, hist, wrow)
-    crosses = lax.all_to_all(cross, (ROWS, COLS), split_axis=0, concat_axis=0, axis_index_groups=[list(range(127, -1, -1))], tiled=True)
-    other = swapped(total, 1)
-    total = total + other
-    gram = total[:, feats:]
-    total = total[:, :feats]
+    other = swapped(packed, 1)
+    cross, total, gram = pl.pallas_call(
+        spread_kernel,
+        in_specs=[VM] * 2,
+        out_specs=[HB, VM, VM],
+        out_shape=[
+            jax.ShapeDtypeStruct((8, 8, 128), f32),
+            pltpu.VMEM((1, feats), f32),
+            pltpu.VMEM((1, 512), f32),
+        ],
+        scratch_shapes=[pltpu.VMEM((8, 8, 128), f32), pltpu.SemaphoreType.DMA],
+        compiler_params=SMALL,
+        name="spread",
+    )(packed, other)
+    crosses = lax.all_to_all(cross.reshape(64, 1, 128), ("x", COLS), split_axis=0, concat_axis=0, axis_index_groups=[list(range(63, -1, -1))], tiled=True)
     other = swapped(total, 3)
     total = total + other
-    other = swapped(total, 7)
+    other = swapped(total, 6)
     solve = pl.pallas_call(
         solve_kernel,
         in_specs=[pl.BlockSpec(memory_space=pltpu.SMEM), VM],
@@ -203,29 +214,22 @@
         compiler_params=SMALL,
         name="solve",
     )(counter, gram)
-    gradient, base = pl.pallas_call(
-        gradient_kernel,
-        in_specs=[VM] * 4,
+    new_weights, gradient = pl.pallas_call(
+        last_kernel,
+        in_specs=[VM] * 6,
         out_specs=[VM] * 2,
-        out_shape=[pltpu.VMEM((1, feats), f32), pltpu.VMEM((1, feats), f32)],
-        compiler_params=SMALL,
-        name="gradient",
-    )(total, other, solve, wrow)
-    new_weights = pl.pallas_call(
-        last_kernel,
-        in_specs=[VM] * 4,
-        out_specs=VM,
-        out_shape=jax.ShapeDtypeStruct((1, feats), f32),
+        out_shape=[jax.ShapeDtypeStruct((1, feats), f32)] * 2,
         compiler_params=SMALL,
         name="last",
-    )(crosses.reshape(16, 8, 128), solve, base, hist)
+    )(crosses.reshape(8, 8, 128), solve, total, other, wrow, hist)
     return new_weights.reshape(feats), gradient.reshape(feats)
 
 
 def solution(mesh):
+    split = Mesh(mesh.devices.reshape(4, 2, 16), ("x", "core", COLS))
     return jax.shard_map(
         body,
-        mesh=mesh,
+        mesh=split,
         in_specs=(P(ROWS, COLS), P(ROWS), P(COLS), P(None, COLS), P(None, COLS), P()),
         out_specs=(P(COLS), P(COLS)),
         check_vma=False,

time: 39 us -> 36.4 us (0.933)
  waiting for transfers between devices: 5.21 us -> 3.48 us
  local copies, waits for them, and re-layouts: 0.62 us -> 0.01 us
    ppermute x3, starting transfers between devices: 5.75 us -> 2.9 us  [swapped(): return lax.ppermute(array, ROWS, [(i, i ^ mask) for i in range(count)])]
    all_to_all x1, starting transfers between devices: 6.77 us -> 9.35 us  [body(): lax.all_to_all(cross.reshape(64, 1, 128), ('x', COLS), split_axis=0, conc...]
    all_to_all x1, waiting for transfers between devices: 3.98 us -> 2.16 us  [body(): lax.all_to_all(cross.reshape(64, 1, 128), ('x', COLS), split_axis=0, conc...]
    unnamed x3 -> x2, local copies, waits for them, and re-layouts: 0.61 us -> 0.01 us
  transfers between devices with their start and end apart: 4 -> 4, of which waited for: 3 -> 3; matrix products, arithmetic and copies ran while one was open for 2% -> 0% of each run, Pallas kernels for 2% -> 2%
where the time goes in v7:
time: 36.4 us; the launch traced here: 36 us
  blocking collectives  12.8 us (35%)
  starting transfers between devices  12.2 us (34%)
  Pallas kernels  6.12 us (17%)
  waiting for transfers between devices  3.48 us (10%)
  between operations  1.34 us (4%)
    all_to_all x1, blocking collectives, body(): lax.all_to_all(part, COLS, split_axis=0, concat_axis=0, axis_index_groups...  12.8 us
    all_to_all x1, starting transfers between devices, body(): lax.all_to_all(cross.reshape(64, 1, 128), ('x', COLS), split_axis=0, conc...  9.35 us
    pallas_call x1, Pallas kernels, body(): pl.pallas_call(first_kernel, in_specs=[HB] * 4, out_specs=[VM] * 4, out_s...  3.14 us
    ppermute x3, starting transfers between devices, swapped(): return lax.ppermute(array, ROWS, [(i, i ^ mask) for i in range(count)])  2.9 us
    all_to_all x1, waiting for transfers between devices, body(): lax.all_to_all(cross.reshape(64, 1, 128), ('x', COLS), split_axis=0, conc...  2.16 us
    ppermute x3, waiting for transfers between devices, swapped(): return lax.ppermute(array, ROWS, [(i, i ^ mask) for i in range(count)])  1.32 us
    pallas_call x1, Pallas kernels, body(): pl.pallas_call(solve_kernel, in_specs=[pl.BlockSpec(memory_space=pltpu.SM...  0.8 us
    pallas_call x1, Pallas kernels, body(): pl.pallas_call(last_kernel, in_specs=[VM] * 6, out_specs=[VM] * 2, out_sh...  0.8 us
  transfers between devices with their start and end apart: 4, of which 3 were waited for; matrix products, arithmetic and copies ran while one was open for 0% of the time, Pallas kernels for 2%

profile of v7, /device:TPU:1, one launch (start us, length us, event | category | flops | bytes accessed | tf_op | source)
XLA Modules:
  0.0 36.0 jit_solution(16295192636385293524)
XLA Ops:
  0.6 0.0 copy-start
  0.6 3.1 %first.1 = (bf16[512,4096]{1,0:T(8,128)(2,1)S(1)}, f32[32,4096]{1,0:T(8,128)S(1)}, f32[1,4096]{1,0:T(1,128)S(1)}, f32[16,8,128]{2,1,0:T(8,128)S(1)}) custom-call(bf16[512,4096]{1,0:T(8,128)(2,1)} %s_hbm.1, f32[1,4096]{1,0:T(1,128)} %bitcast.10, f32[16,4096]{1,0:T(8,128)} %hs_hbm.1, f32[16,4096]{1,0:T(8,128)} %hy_hbm.1), custom_call_target="tpu_custom_call" | custom-call | tf_op jit(solution)/shard_map/first/pallas_call | solution.py:168
  3.8 12.8 %all_to_all.10.parts = f32[16,8,128]{2,1,0:T(8,128)S(1)} all-to-all(f32[16,8,128]{2,1,0:T(8,128)S(1)} %get-tuple-element.11), channel_id=1, replica_groups={{15,0,1,2,3,4,5,6,7,8,9,10,11,12,13,14},{31,16,17,18,19,20,21,22,23,24,..., dimensions={0} | all-to-all | bytes 131072 | tf_op jit(solution)/shard_map/all_to_all | solution.py:182
  16.6 0.0 copy-done
  16.6 0.8 %second.1.mine = f32[1,4736]{1,0:T(1,128)S(1)} custom-call(f32[16,8,128]{2,1,0:T(8,128)S(1)} %all_to_all.10.parts, s32[1,512]{1,0:T(1,128)S(1)} %bitcast.9, bf16[512,4096]{1,0:T(8,128)(2,1)S(1)} %get-tuple-element.12.samp, f32[32,4096]{1,0:T(8,128)S(1)} %get-tuple-element.13.hist, f32[1,4096]{1,0:T(1,128)S(1)} %get-tuple-element.14.wrow), custom_call_target="tpu_custom_call" | custom-call | tf_op jit(solution)/shard_map/second/pallas_call | solution.py:183
  17.4 1.3 %collective-permute-start = (f32[1,4736]{1,0:T(1,128)S(1)}, f32[1,4736]{1,0:T(1,128)S(1)}, u32[]{:S(2)}, u32[]{:S(2)}) collective-permute-start(f32[1,4736]{1,0:T(1,128)S(1)} %second.1.mine), channel_id=1, source_target_pairs={{0,16},{16,0},{32,48},{48,32},{64,80},{80,64},{96,112},{112,96},{1... | collective-permute-start | bytes 56840 | tf_op jit(solution)/shard_map/ppermute | solution.py:158
  18.7 0.8 %collective-permute-done.other = f32[1,4736]{1,0:T(1,128)S(1)} collective-permute-done((f32[1,4736]{1,0:T(1,128)S(1)}, f32[1,4736]{1,0:T(1,128)S(1)}, u32[]{:S(2)}, u32[]{:S(2)}) %collective-permute-start) | collective-permute-done | bytes 18976 | tf_op jit(solution)/shard_map/ppermute | solution.py:158
  19.5 0.6 %spread.1 = (f32[8,8,128]{2,1,0:T(8,128)}, f32[1,4096]{1,0:T(1,128)S(1)}, f32[1,512]{1,0:T(1,128)S(1)}) custom-call(f32[1,4736]{1,0:T(1,128)S(1)} %second.1.mine, f32[1,4736]{1,0:T(1,128)S(1)} %collective-permute-done.other), custom_call_target="tpu_custom_call" | custom-call | tf_op jit(solution)/shard_map/spread/pallas_call | solution.py:192
  20.1 1.5 %collective-permute-start.1 = (f32[1,4096]{1,0:T(1,128)S(1)}, f32[1,4096]{1,0:T(1,128)S(1)}, u32[]{:S(2)}, u32[]{:S(2)}) collective-permute-start(f32[1,4096]{1,0:T(1,128)S(1)} %get-tuple-element.17), channel_id=1, source_target_pairs={{0,48},{16,32},{32,16},{48,0},{64,112},{80,96},{96,80},{112,64},{1... | collective-permute-start | bytes 49160 | tf_op jit(solution)/shard_map/ppermute | solution.py:158
  21.7 9.3 %all-to-all-start.1 = ((f32[64,1,128]{2,1,0:T(1,128)}), f32[64,1,128]{2,1,0:T(1,128)S(1)}, u32[]{:S(2)}, u32[]{:S(2)}) async-start(f32[64,1,128]{2,1,0:T(1,128)} %bitcast.3), calls=%async_computation.1 | async-start | bytes 65536 | tf_op jit(solution)/shard_map/all_to_all | solution.py:205
  31.0 0.0 collective-permute-done.1
  31.1 0.1 collective-permute-start.2
  31.8 0.8 %solve.1 = f32[40,128]{1,0:T(8,128)S(1)} custom-call(s32[1]{0:T(128)S(6)} %copy.9.counter, f32[1,512]{1,0:T(1,128)S(1)} %get-tuple-element.16.gram), custom_call_target="tpu_custom_call" | custom-call | tf_op jit(solution)/shard_map/solve/pallas_call | solution.py:209
  32.6 2.2 %all-to-all-done.1 = f32[64,1,128]{2,1,0:T(1,128)S(1)} async-done(((f32[64,1,128]{2,1,0:T(1,128)}), f32[64,1,128]{2,1,0:T(1,128)S(1)}, u32[]{:S(2)}, u32[]{:S(2)}) %all-to-all-start.1) | async-done | bytes 32800 | tf_op jit(solution)/shard_map/all_to_all | solution.py:205
  34.8 0.5 %collective-permute-done.2.other = f32[1,4096]{1,0:T(1,128)S(1)} collective-permute-done((f32[1,4096]{1,0:T(1,128)S(1)}, f32[1,4096]{1,0:T(1,128)S(1)}, u32[]{:S(2)}, u32[]{:S(2)}) %collective-permute-start.2) | collective-permute-done | bytes 16416 | tf_op jit(solution)/shard_map/ppermute | solution.py:158
  35.2 0.8 %last.1 = (f32[1,4096]{1,0:T(1,128)}, f32[1,4096]{1,0:T(1,128)}) custom-call(f32[8,8,128]{2,1,0:T(8,128)S(1)} %bitcast.8, f32[40,128]{1,0:T(8,128)S(1)} %solve.1, f32[1,4096]{1,0:T(1,128)S(1)} %add.3.mine, f32[1,4096]{1,0:T(1,128)S(1)} %collective-permute-done.2.other, f32[1,4096]{1,0:T(1,128)S(1)} %get-tuple-element.14.wrow, ...), custom_call_target="tpu_custom_call" | custom-call | tf_op jit(solution)/shard_map/last/pallas_call | solution.py:217
  (1 shorter events, 0.0 us)
Async XLA Ops:
  0.6 16.0 %copy-start = (s32[512]{0:T(512)S(1)}, s32[512]{0:T(512)}, u32[]{:S(2)}) copy-start(s32[512]{0:T(512)} %param.7) | copy-start | bytes 6148
  17.4 2.1 %collective-permute-start = (f32[1,4736]{1,0:T(1,128)S(1)}, f32[1,4736]{1,0:T(1,128)S(1)}, u32[]{:S(2)}, u32[]{:S(2)}) collective-permute-start(f32[1,4736]{1,0:T(1,128)S(1)} %second.1.mine), channel_id=1, source_target_pairs={{0,16},{16,0},{32,48},{48,32},{64,80},{80,64},{96,112},{112,96},{1... | collective-permute-start | bytes 56840 | tf_op jit(solution)/shard_map/ppermute | solution.py:158
  20.1 10.9 %collective-permute-start.1 = (f32[1,4096]{1,0:T(1,128)S(1)}, f32[1,4096]{1,0:T(1,128)S(1)}, u32[]{:S(2)}, u32[]{:S(2)}) collective-permute-start(f32[1,4096]{1,0:T(1,128)S(1)} %get-tuple-element.17), channel_id=1, source_target_pairs={{0,48},{16,32},{32,16},{48,0},{64,112},{80,96},{96,80},{112,64},{1... | collective-permute-start | bytes 49160 | tf_op jit(solution)/shard_map/ppermute | solution.py:158
  21.7 13.1 %all-to-all-start.1 = ((f32[64,1,128]{2,1,0:T(1,128)}), f32[64,1,128]{2,1,0:T(1,128)S(1)}, u32[]{:S(2)}, u32[]{:S(2)}) async-start(f32[64,1,128]{2,1,0:T(1,128)} %bitcast.3), calls=%async_computation.1 | async-start | bytes 65536 | tf_op jit(solution)/shard_map/all_to_all | solution.py:205
  31.1 4.2 %collective-permute-start.2 = (f32[1,4096]{1,0:T(1,128)S(1)}, f32[1,4096]{1,0:T(1,128)S(1)}, u32[]{:S(2)}, u32[]{:S(2)}) collective-permute-start(f32[1,4096]{1,0:T(1,128)S(1)} %add.3.mine), channel_id=1, source_target_pairs={{0,96},{16,112},{32,64},{48,80},{64,32},{80,48},{96,0},{112,16},{1... | collective-permute-start | bytes 49160 | tf_op jit(solution)/shard_map/ppermute | solution.py:158

commit v8 on v7

--- a/solution.py
+++ b/solution.py
@@ -10,7 +10,7 @@
 HIST = 16
 ROWS = ("x", "core")
 COLS = "cols"
-CHUNKS = 8
+CHUNKS = 16
 
 penalty = 4.0
 step_length = 0.5
@@ -79,9 +79,9 @@
     margin = jnp.concatenate([summed[i : i + 1] for i in range(4)], axis=1)
     resid = (jax.nn.sigmoid(margin) - labels[...].astype(f32)).astype(bf16)
     resid16 = jnp.broadcast_to(resid, (16, resid.shape[1]))
-    width = feats // CHUNKS
+    width = 1024
     acc = jnp.zeros((2 * HIST, 128), f32)
-    for c in range(CHUNKS):
+    for c in range(feats // width):
         cols = slice(c * width, (c + 1) * width)
         t = jnp.dot(resid16, samp[:, cols], preferred_element_type=f32)[0:1]
         packed[:, cols] = t
@@ -89,8 +89,9 @@
         prod = hist[:, cols] * lead
         for k in range(width // 128):
             acc = acc + prod[:, 128 * k : 128 * k + 128]
-    square = jnp.concatenate([acc, jnp.zeros((128 - 2 * HIST, 128), f32)], axis=0)
-    packed[:, feats + 512 :] = jnp.sum(square.T, axis=0, keepdims=True)
+    sums = jnp.sum(acc, axis=1, keepdims=True)
+    here = iota(acc.shape, 0) == iota(acc.shape, 1)
+    packed[:, feats + 512 :] = jnp.sum(jnp.where(here, sums, 0.0), axis=0, keepdims=True)
 
 
 def spread_kernel(mine, other, cross_hbm, total, gram, cross, sem):
@@ -179,7 +180,7 @@
         compiler_params=SMALL,
         name="first",
     )(*(pltpu.with_memory_space_constraint(a, pltpu.HBM) for a in (samples, weights.reshape(1, feats), hist_s, hist_y)))
-    parts = lax.all_to_all(part, COLS, split_axis=0, concat_axis=0, axis_index_groups=[[15] + list(range(15))], tiled=True)
+    parts = lax.all_to_all(part, COLS, split_axis=0, concat_axis=0, axis_index_groups=[list(range(15, -1, -1))], tiled=True)
     packed = pl.pallas_call(
         second_kernel,
         in_specs=[VM] * 5,
@@ -202,7 +203,7 @@
         compiler_params=SMALL,
         name="spread",
     )(packed, other)
-    crosses = lax.all_to_all(cross.reshape(64, 1, 128), ("x", COLS), split_axis=0, concat_axis=0, axis_index_groups=[list(range(63, -1, -1))], tiled=True)
+    crosses = lax.all_to_all(cross.reshape(64, 1, 128), ("x", COLS), split_axis=0, concat_axis=0, axis_index_groups=[[63] + list(range(63))], tiled=True)
     other = swapped(total, 3)
     total = total + other
     other = swapped(total, 6)

time: 36.4 us -> 36 us (0.989)
  waiting for transfers between devices: 3.48 us -> 2.99 us
    ppermute x3, starting transfers between devices: 2.9 us -> 3.37 us  [swapped(): return lax.ppermute(array, ROWS, [(i, i ^ mask) for i in range(count)])]
where the time goes in v8:
time: 36 us; the launch traced here: 35.6 us
  blocking collectives  12.8 us (36%)
  starting transfers between devices  12.4 us (34%)
  Pallas kernels  6.13 us (17%)
  waiting for transfers between devices  2.99 us (8%)
  between operations  1.33 us (4%)
    all_to_all x1, blocking collectives, body(): lax.all_to_all(part, COLS, split_axis=0, concat_axis=0, axis_index_groups...  12.8 us
    all_to_all x1, starting transfers between devices, body(): lax.all_to_all(cross.reshape(64, 1, 128), ('x', COLS), split_axis=0, conc...  9.03 us
    ppermute x3, starting transfers between devices, swapped(): return lax.ppermute(array, ROWS, [(i, i ^ mask) for i in range(count)])  3.37 us
    pallas_call x1, Pallas kernels, body(): pl.pallas_call(first_kernel, in_specs=[HB] * 4, out_specs=[VM] * 4, out_s...  3.15 us
    all_to_all x1, waiting for transfers between devices, body(): lax.all_to_all(cross.reshape(64, 1, 128), ('x', COLS), split_axis=0, conc...  1.93 us
    ppermute x3, waiting for transfers between devices, swapped(): return lax.ppermute(array, ROWS, [(i, i ^ mask) for i in range(count)])  1.06 us
    pallas_call x1, Pallas kernels, body(): pl.pallas_call(solve_kernel, in_specs=[pl.BlockSpec(memory_space=pltpu.SM...  0.8 us
    pallas_call x1, Pallas kernels, body(): pl.pallas_call(last_kernel, in_specs=[VM] * 6, out_specs=[VM] * 2, out_sh...  0.8 us
  transfers between devices with their start and end apart: 4, of which 3 were waited for; matrix products, arithmetic and copies ran while one was open for 0% of the time, Pallas kernels for 2%

profile of v8, /device:TPU:1, one launch (start us, length us, event | category | flops | bytes accessed | tf_op | source)
XLA Modules:
  0.0 35.6 jit_solution(16939937286648295750)
XLA Ops:
  0.6 0.0 copy-start
  0.6 3.2 %first.1 = (bf16[512,4096]{1,0:T(8,128)(2,1)S(1)}, f32[32,4096]{1,0:T(8,128)S(1)}, f32[1,4096]{1,0:T(1,128)S(1)}, f32[16,8,128]{2,1,0:T(8,128)S(1)}) custom-call(bf16[512,4096]{1,0:T(8,128)(2,1)} %s_hbm.1, f32[1,4096]{1,0:T(1,128)} %bitcast.10, f32[16,4096]{1,0:T(8,128)} %hs_hbm.1, f32[16,4096]{1,0:T(8,128)} %hy_hbm.1), custom_call_target="tpu_custom_call" | custom-call | tf_op jit(solution)/shard_map/first/pallas_call | solution.py:169
  3.8 12.8 %all_to_all.10.parts = f32[16,8,128]{2,1,0:T(8,128)S(1)} all-to-all(f32[16,8,128]{2,1,0:T(8,128)S(1)} %get-tuple-element.11), channel_id=1, replica_groups={{15,14,13,12,11,10,9,8,7,6,5,4,3,2,1,0},{31,30,29,28,27,26,25,24,23,22,..., dimensions={0} | all-to-all | bytes 131072 | tf_op jit(solution)/shard_map/all_to_all | solution.py:183
  16.6 0.0 copy-done
  16.6 0.8 %second.1.mine = f32[1,4736]{1,0:T(1,128)S(1)} custom-call(f32[16,8,128]{2,1,0:T(8,128)S(1)} %all_to_all.10.parts, s32[1,512]{1,0:T(1,128)S(1)} %bitcast.9, bf16[512,4096]{1,0:T(8,128)(2,1)S(1)} %get-tuple-element.12.samp, f32[32,4096]{1,0:T(8,128)S(1)} %get-tuple-element.13.hist, f32[1,4096]{1,0:T(1,128)S(1)} %get-tuple-element.14.wrow), custom_call_target="tpu_custom_call" | custom-call | tf_op jit(solution)/shard_map/second/pallas_call | solution.py:184
  17.3 1.3 %collective-permute-start = (f32[1,4736]{1,0:T(1,128)S(1)}, f32[1,4736]{1,0:T(1,128)S(1)}, u32[]{:S(2)}, u32[]{:S(2)}) collective-permute-start(f32[1,4736]{1,0:T(1,128)S(1)} %second.1.mine), channel_id=1, source_target_pairs={{0,16},{16,0},{32,48},{48,32},{64,80},{80,64},{96,112},{112,96},{1... | collective-permute-start | bytes 56840 | tf_op jit(solution)/shard_map/ppermute | solution.py:159
  18.6 0.8 %collective-permute-done.other = f32[1,4736]{1,0:T(1,128)S(1)} collective-permute-done((f32[1,4736]{1,0:T(1,128)S(1)}, f32[1,4736]{1,0:T(1,128)S(1)}, u32[]{:S(2)}, u32[]{:S(2)}) %collective-permute-start) | collective-permute-done | bytes 18976 | tf_op jit(solution)/shard_map/ppermute | solution.py:159
  19.4 0.6 %spread.1 = (f32[8,8,128]{2,1,0:T(8,128)}, f32[1,4096]{1,0:T(1,128)S(1)}, f32[1,512]{1,0:T(1,128)S(1)}) custom-call(f32[1,4736]{1,0:T(1,128)S(1)} %second.1.mine, f32[1,4736]{1,0:T(1,128)S(1)} %collective-permute-done.other), custom_call_target="tpu_custom_call" | custom-call | tf_op jit(solution)/shard_map/spread/pallas_call | solution.py:193
  20.1 1.5 %collective-permute-start.1 = (f32[1,4096]{1,0:T(1,128)S(1)}, f32[1,4096]{1,0:T(1,128)S(1)}, u32[]{:S(2)}, u32[]{:S(2)}) collective-permute-start(f32[1,4096]{1,0:T(1,128)S(1)} %get-tuple-element.17), channel_id=1, source_target_pairs={{0,48},{16,32},{32,16},{48,0},{64,112},{80,96},{96,80},{112,64},{1... | collective-permute-start | bytes 49160 | tf_op jit(solution)/shard_map/ppermute | solution.py:159
  21.6 9.0 %all-to-all-start.1 = ((f32[64,1,128]{2,1,0:T(1,128)}), f32[64,1,128]{2,1,0:T(1,128)S(1)}, u32[]{:S(2)}, u32[]{:S(2)}) async-start(f32[64,1,128]{2,1,0:T(1,128)} %bitcast.3), calls=%async_computation.1 | async-start | bytes 65536 | tf_op jit(solution)/shard_map/all_to_all | solution.py:206
  30.6 0.0 collective-permute-done.1
  30.7 0.6 %collective-permute-start.2 = (f32[1,4096]{1,0:T(1,128)S(1)}, f32[1,4096]{1,0:T(1,128)S(1)}, u32[]{:S(2)}, u32[]{:S(2)}) collective-permute-start(f32[1,4096]{1,0:T(1,128)S(1)} %add.3.mine), channel_id=1, source_target_pairs={{0,96},{16,112},{32,64},{48,80},{64,32},{80,48},{96,0},{112,16},{1... | collective-permute-start | bytes 49160 | tf_op jit(solution)/shard_map/ppermute | solution.py:159
  31.9 0.8 %solve.1 = f32[40,128]{1,0:T(8,128)S(1)} custom-call(s32[1]{0:T(128)S(6)} %copy.9.counter, f32[1,512]{1,0:T(1,128)S(1)} %get-tuple-element.16.gram), custom_call_target="tpu_custom_call" | custom-call | tf_op jit(solution)/shard_map/solve/pallas_call | solution.py:210
  32.7 1.9 %all-to-all-done.1 = f32[64,1,128]{2,1,0:T(1,128)S(1)} async-done(((f32[64,1,128]{2,1,0:T(1,128)}), f32[64,1,128]{2,1,0:T(1,128)S(1)}, u32[]{:S(2)}, u32[]{:S(2)}) %all-to-all-start.1) | async-done | bytes 32800 | tf_op jit(solution)/shard_map/all_to_all | solution.py:206
  34.6 0.2 collective-permute-done.2.other
  34.8 0.8 %last.1 = (f32[1,4096]{1,0:T(1,128)}, f32[1,4096]{1,0:T(1,128)}) custom-call(f32[8,8,128]{2,1,0:T(8,128)S(1)} %bitcast.8, f32[40,128]{1,0:T(8,128)S(1)} %solve.1, f32[1,4096]{1,0:T(1,128)S(1)} %add.3.mine, f32[1,4096]{1,0:T(1,128)S(1)} %collective-permute-done.2.other, f32[1,4096]{1,0:T(1,128)S(1)} %get-tuple-element.14.wrow, ...), custom_call_target="tpu_custom_call" | custom-call | tf_op jit(solution)/shard_map/last/pallas_call | solution.py:218
  (1 shorter events, 0.0 us)
Async XLA Ops:
  0.6 15.9 %copy-start = (s32[512]{0:T(512)S(1)}, s32[512]{0:T(512)}, u32[]{:S(2)}) copy-start(s32[512]{0:T(512)} %param.7) | copy-start | bytes 6148
  17.3 2.1 %collective-permute-start = (f32[1,4736]{1,0:T(1,128)S(1)}, f32[1,4736]{1,0:T(1,128)S(1)}, u32[]{:S(2)}, u32[]{:S(2)}) collective-permute-start(f32[1,4736]{1,0:T(1,128)S(1)} %second.1.mine), channel_id=1, source_target_pairs={{0,16},{16,0},{32,48},{48,32},{64,80},{80,64},{96,112},{112,96},{1... | collective-permute-start | bytes 56840 | tf_op jit(solution)/shard_map/ppermute | solution.py:159
  20.1 10.6 %collective-permute-start.1 = (f32[1,4096]{1,0:T(1,128)S(1)}, f32[1,4096]{1,0:T(1,128)S(1)}, u32[]{:S(2)}, u32[]{:S(2)}) collective-permute-start(f32[1,4096]{1,0:T(1,128)S(1)} %get-tuple-element.17), channel_id=1, source_target_pairs={{0,48},{16,32},{32,16},{48,0},{64,112},{80,96},{96,80},{112,64},{1... | collective-permute-start | bytes 49160 | tf_op jit(solution)/shard_map/ppermute | solution.py:159
  21.6 13.0 %all-to-all-start.1 = ((f32[64,1,128]{2,1,0:T(1,128)}), f32[64,1,128]{2,1,0:T(1,128)S(1)}, u32[]{:S(2)}, u32[]{:S(2)}) async-start(f32[64,1,128]{2,1,0:T(1,128)} %bitcast.3), calls=%async_computation.1 | async-start | bytes 65536 | tf_op jit(solution)/shard_map/all_to_all | solution.py:206
  30.7 4.2 %collective-permute-start.2 = (f32[1,4096]{1,0:T(1,128)S(1)}, f32[1,4096]{1,0:T(1,128)S(1)}, u32[]{:S(2)}, u32[]{:S(2)}) collective-permute-start(f32[1,4096]{1,0:T(1,128)S(1)} %add.3.mine), channel_id=1, source_target_pairs={{0,96},{16,112},{32,64},{48,80},{64,32},{80,48},{96,0},{112,16},{1... | collective-permute-start | bytes 49160 | tf_op jit(solution)/shard_map/ppermute | solution.py:159

commit v9 on v8

--- a/solution.py
+++ b/solution.py
@@ -144,14 +144,25 @@
     out[2 * HIST :, :] = jnp.broadcast_to(gamma, (8, 128))
 
 
-def last_kernel(crosses, solve, mine, other, wrow, hist, new_weights, gradient):
-    line = jnp.sum(jnp.sum(crosses[...], axis=0), axis=0, keepdims=True)
-    coefs = step_length * jnp.sum(solve[0 : 2 * HIST, :] * line, axis=1, keepdims=True)
+def last_kernel(crosses, solve, mine, other, wrow, hist, new_hbm, grad_hbm, new, gradient, sems):
+    feats = wrow.shape[1]
     weights = wrow[...]
     grad = weights + penalty * (mine[...] + other[...])
     gradient[...] = grad
-    base = weights - (step_length * solve[2 * HIST : 2 * HIST + 1, 0:1]) * grad
-    new_weights[...] = base - jnp.sum(hist[...] * coefs, axis=0, keepdims=True)
+    outs = [pltpu.make_async_copy(gradient, grad_hbm, sems.at[0])]
+    outs[0].start()
+    line = jnp.sum(jnp.sum(crosses[...], axis=0), axis=0, keepdims=True)
+    coefs = step_length * jnp.sum(solve[0 : 2 * HIST, :] * line, axis=1, keepdims=True)
+    gamma = step_length * solve[2 * HIST : 2 * HIST + 1, 0:1]
+    for i in range(2):
+        cols = slice(i * feats // 2, (i + 1) * feats // 2)
+        mixed = jnp.sum(hist[:, cols] * coefs, axis=0, keepdims=True)
+        new[:, cols] = wrow[:, cols] - gamma * grad[:, cols] - mixed
+        half = pl.ds(i * feats // 2, feats // 2)
+        outs.append(pltpu.make_async_copy(new.at[:, half], new_hbm.at[:, half], sems.at[1 + i]))
+        outs[-1].start()
+    for out in outs:
+        out.wait()
 
 
 def swapped(array, mask):
@@ -218,8 +229,9 @@
     new_weights, gradient = pl.pallas_call(
         last_kernel,
         in_specs=[VM] * 6,
-        out_specs=[VM] * 2,
+        out_specs=[HB] * 2,
         out_shape=[jax.ShapeDtypeStruct((1, feats), f32)] * 2,
+        scratch_shapes=[pltpu.VMEM((1, feats), f32), pltpu.VMEM((1, feats), f32), pltpu.SemaphoreType.DMA((3,))],
         compiler_params=SMALL,
         name="last",
     )(crosses.reshape(8, 8, 128), solve, total, other, wrow, hist)

time: 36 us -> 36.1 us (level)
  no operation moved by 1% of the time
where the time goes in v9:
time: 36.1 us; the launch traced here: 35.7 us
  blocking collectives  12.8 us (35%)
  starting transfers between devices  12.4 us (34%)
  Pallas kernels  6.14 us (17%)
  waiting for transfers between devices  2.99 us (8%)
  between operations  1.33 us (4%)
    all_to_all x1, blocking collectives, body(): lax.all_to_all(part, COLS, split_axis=0, concat_axis=0, axis_index_groups...  12.8 us
    all_to_all x1, starting transfers between devices, body(): lax.all_to_all(cross.reshape(64, 1, 128), ('x', COLS), split_axis=0, conc...  9.03 us
    ppermute x3, starting transfers between devices, swapped(): return lax.ppermute(array, ROWS, [(i, i ^ mask) for i in range(count)])  3.37 us
    pallas_call x1, Pallas kernels, body(): pl.pallas_call(first_kernel, in_specs=[HB] * 4, out_specs=[VM] * 4, out_s...  3.15 us
    all_to_all x1, waiting for transfers between devices, body(): lax.all_to_all(cross.reshape(64, 1, 128), ('x', COLS), split_axis=0, conc...  1.93 us
    ppermute x3, waiting for transfers between devices, swapped(): return lax.ppermute(array, ROWS, [(i, i ^ mask) for i in range(count)])  1.06 us
    pallas_call x1, Pallas kernels, body(): pl.pallas_call(last_kernel, in_specs=[VM] * 6, out_specs=[HB] * 2, out_sh...  0.81 us
    pallas_call x1, Pallas kernels, body(): pl.pallas_call(solve_kernel, in_specs=[pl.BlockSpec(memory_space=pltpu.SM...  0.8 us
  transfers between devices with their start and end apart: 4, of which 3 were waited for; matrix products, arithmetic and copies ran while one was open for 0% of the time, Pallas kernels for 2%

profile of v9, /device:TPU:1, one launch (start us, length us, event | category | flops | bytes accessed | tf_op | source)
XLA Modules:
  0.0 35.7 jit_solution(9993532740761185059)
XLA Ops:
  0.6 0.0 copy-start
  0.6 3.2 %first.1 = (bf16[512,4096]{1,0:T(8,128)(2,1)S(1)}, f32[32,4096]{1,0:T(8,128)S(1)}, f32[1,4096]{1,0:T(1,128)S(1)}, f32[16,8,128]{2,1,0:T(8,128)S(1)}) custom-call(bf16[512,4096]{1,0:T(8,128)(2,1)} %s_hbm.1, f32[1,4096]{1,0:T(1,128)} %bitcast.10, f32[16,4096]{1,0:T(8,128)} %hs_hbm.1, f32[16,4096]{1,0:T(8,128)} %hy_hbm.1), custom_call_target="tpu_custom_call" | custom-call | tf_op jit(solution)/shard_map/first/pallas_call | solution.py:180
  3.8 12.8 %all_to_all.10.parts = f32[16,8,128]{2,1,0:T(8,128)S(1)} all-to-all(f32[16,8,128]{2,1,0:T(8,128)S(1)} %get-tuple-element.11), channel_id=1, replica_groups={{15,14,13,12,11,10,9,8,7,6,5,4,3,2,1,0},{31,30,29,28,27,26,25,24,23,22,..., dimensions={0} | all-to-all | bytes 131072 | tf_op jit(solution)/shard_map/all_to_all | solution.py:194
  16.6 0.0 copy-done
  16.6 0.8 %second.1.mine = f32[1,4736]{1,0:T(1,128)S(1)} custom-call(f32[16,8,128]{2,1,0:T(8,128)S(1)} %all_to_all.10.parts, s32[1,512]{1,0:T(1,128)S(1)} %bitcast.9, bf16[512,4096]{1,0:T(8,128)(2,1)S(1)} %get-tuple-element.12.samp, f32[32,4096]{1,0:T(8,128)S(1)} %get-tuple-element.13.hist, f32[1,4096]{1,0:T(1,128)S(1)} %get-tuple-element.14.wrow), custom_call_target="tpu_custom_call" | custom-call | tf_op jit(solution)/shard_map/second/pallas_call | solution.py:195
  17.3 1.3 %collective-permute-start = (f32[1,4736]{1,0:T(1,128)S(1)}, f32[1,4736]{1,0:T(1,128)S(1)}, u32[]{:S(2)}, u32[]{:S(2)}) collective-permute-start(f32[1,4736]{1,0:T(1,128)S(1)} %second.1.mine), channel_id=1, source_target_pairs={{0,16},{16,0},{32,48},{48,32},{64,80},{80,64},{96,112},{112,96},{1... | collective-permute-start | bytes 56840 | tf_op jit(solution)/shard_map/ppermute | solution.py:170
  18.6 0.8 %collective-permute-done.other = f32[1,4736]{1,0:T(1,128)S(1)} collective-permute-done((f32[1,4736]{1,0:T(1,128)S(1)}, f32[1,4736]{1,0:T(1,128)S(1)}, u32[]{:S(2)}, u32[]{:S(2)}) %collective-permute-start) | collective-permute-done | bytes 18976 | tf_op jit(solution)/shard_map/ppermute | solution.py:170
  19.4 0.6 %spread.1 = (f32[8,8,128]{2,1,0:T(8,128)}, f32[1,4096]{1,0:T(1,128)S(1)}, f32[1,512]{1,0:T(1,128)S(1)}) custom-call(f32[1,4736]{1,0:T(1,128)S(1)} %second.1.mine, f32[1,4736]{1,0:T(1,128)S(1)} %collective-permute-done.other), custom_call_target="tpu_custom_call" | custom-call | tf_op jit(solution)/shard_map/spread/pallas_call | solution.py:204
  20.1 1.5 %collective-permute-start.1 = (f32[1,4096]{1,0:T(1,128)S(1)}, f32[1,4096]{1,0:T(1,128)S(1)}, u32[]{:S(2)}, u32[]{:S(2)}) collective-permute-start(f32[1,4096]{1,0:T(1,128)S(1)} %get-tuple-element.17), channel_id=1, source_target_pairs={{0,48},{16,32},{32,16},{48,0},{64,112},{80,96},{96,80},{112,64},{1... | collective-permute-start | bytes 49160 | tf_op jit(solution)/shard_map/ppermute | solution.py:170
  21.6 9.0 %all-to-all-start.1 = ((f32[64,1,128]{2,1,0:T(1,128)}), f32[64,1,128]{2,1,0:T(1,128)S(1)}, u32[]{:S(2)}, u32[]{:S(2)}) async-start(f32[64,1,128]{2,1,0:T(1,128)} %bitcast.3), calls=%async_computation.1 | async-start | bytes 65536 | tf_op jit(solution)/shard_map/all_to_all | solution.py:217
  30.6 0.0 collective-permute-done.1
  30.7 0.6 %collective-permute-start.2 = (f32[1,4096]{1,0:T(1,128)S(1)}, f32[1,4096]{1,0:T(1,128)S(1)}, u32[]{:S(2)}, u32[]{:S(2)}) collective-permute-start(f32[1,4096]{1,0:T(1,128)S(1)} %add.3.mine), channel_id=1, source_target_pairs={{0,96},{16,112},{32,64},{48,80},{64,32},{80,48},{96,0},{112,16},{1... | collective-permute-start | bytes 49160 | tf_op jit(solution)/shard_map/ppermute | solution.py:170
  31.9 0.8 %solve.1 = f32[40,128]{1,0:T(8,128)S(1)} custom-call(s32[1]{0:T(128)S(6)} %copy.9.counter, f32[1,512]{1,0:T(1,128)S(1)} %get-tuple-element.16.gram), custom_call_target="tpu_custom_call" | custom-call | tf_op jit(solution)/shard_map/solve/pallas_call | solution.py:221
  32.7 1.9 %all-to-all-done.1 = f32[64,1,128]{2,1,0:T(1,128)S(1)} async-done(((f32[64,1,128]{2,1,0:T(1,128)}), f32[64,1,128]{2,1,0:T(1,128)S(1)}, u32[]{:S(2)}, u32[]{:S(2)}) %all-to-all-start.1) | async-done | bytes 32800 | tf_op jit(solution)/shard_map/all_to_all | solution.py:217
  34.6 0.2 collective-permute-done.2.other
  34.8 0.8 %last.1 = (f32[1,4096]{1,0:T(1,128)}, f32[1,4096]{1,0:T(1,128)}) custom-call(f32[8,8,128]{2,1,0:T(8,128)S(1)} %bitcast.8, f32[40,128]{1,0:T(8,128)S(1)} %solve.1, f32[1,4096]{1,0:T(1,128)S(1)} %add.3.mine, f32[1,4096]{1,0:T(1,128)S(1)} %collective-permute-done.2.other, f32[1,4096]{1,0:T(1,128)S(1)} %get-tuple-element.14.wrow, ...), custom_call_target="tpu_custom_call" | custom-call | tf_op jit(solution)/shard_map/last/pallas_call | solution.py:229
  (1 shorter events, 0.0 us)
Async XLA Ops:
  0.6 15.9 %copy-start = (s32[512]{0:T(512)S(1)}, s32[512]{0:T(512)}, u32[]{:S(2)}) copy-start(s32[512]{0:T(512)} %param.7) | copy-start | bytes 6148
  17.3 2.1 %collective-permute-start = (f32[1,4736]{1,0:T(1,128)S(1)}, f32[1,4736]{1,0:T(1,128)S(1)}, u32[]{:S(2)}, u32[]{:S(2)}) collective-permute-start(f32[1,4736]{1,0:T(1,128)S(1)} %second.1.mine), channel_id=1, source_target_pairs={{0,16},{16,0},{32,48},{48,32},{64,80},{80,64},{96,112},{112,96},{1... | collective-permute-start | bytes 56840 | tf_op jit(solution)/shard_map/ppermute | solution.py:170
  20.1 10.6 %collective-permute-start.1 = (f32[1,4096]{1,0:T(1,128)S(1)}, f32[1,4096]{1,0:T(1,128)S(1)}, u32[]{:S(2)}, u32[]{:S(2)}) collective-permute-start(f32[1,4096]{1,0:T(1,128)S(1)} %get-tuple-element.17), channel_id=1, source_target_pairs={{0,48},{16,32},{32,16},{48,0},{64,112},{80,96},{96,80},{112,64},{1... | collective-permute-start | bytes 49160 | tf_op jit(solution)/shard_map/ppermute | solution.py:170
  21.6 13.0 %all-to-all-start.1 = ((f32[64,1,128]{2,1,0:T(1,128)}), f32[64,1,128]{2,1,0:T(1,128)S(1)}, u32[]{:S(2)}, u32[]{:S(2)}) async-start(f32[64,1,128]{2,1,0:T(1,128)} %bitcast.3), calls=%async_computation.1 | async-start | bytes 65536 | tf_op jit(solution)/shard_map/all_to_all | solution.py:217
  30.7 4.2 %collective-permute-start.2 = (f32[1,4096]{1,0:T(1,128)S(1)}, f32[1,4096]{1,0:T(1,128)S(1)}, u32[]{:S(2)}, u32[]{:S(2)}) collective-permute-start(f32[1,4096]{1,0:T(1,128)S(1)} %add.3.mine), channel_id=1, source_target_pairs={{0,96},{16,112},{32,64},{48,80},{64,32},{80,48},{96,0},{112,16},{1... | collective-permute-start | bytes 49160 | tf_op jit(solution)/shard_map/ppermute | solution.py:170
